TPU v7x, 256 devices: a whole 4x4x8 slice. The times are simulated.
256 devices in a mesh: row: 8 (over z_lo, y), col: 32 (over z_hi, x, core).
Axes of the slice: x: 4, y: 4, z: 8 (z_hi: 4, z_lo: 2; z = z_hi * 2 + z_lo), core: 2. Of those that a mesh axis runs over, the one named last changes fastest.
Arguments:
- alignment: float32 [512, 768, 256], P('row', 'col'), may hold values from -40 to 40
- seq_mask: int32 [512], replicated, may hold values 0 or 1
- res_mask: int32 [768], replicated, may hold values 0 or 1
- attn_gain: float32 [256], replicated, may hold values from 0.5 to 1.5
- outer_product_gain: float32 [256], replicated, may hold values from 0.5 to 1.5
- w_query: bfloat16 [256, 256], replicated, may hold values from -24 to 24
- w_key: bfloat16 [256, 256], replicated, may hold values from -2 to 2
- w_value: bfloat16 [256, 256], replicated, may hold values from -0.375 to 0.375
- w_gate: bfloat16 [256, 256], replicated, may hold values from -0.375 to 0.375
- output_weight: bfloat16 [256, 256], replicated, may hold values from -0.375 to 0.375
- w_left: bfloat16 [256, 32], replicated, may hold values from -0.375 to 0.375
- w_right: bfloat16 [256, 32], replicated, may hold values from -0.375 to 0.375
- w_pair: bfloat16 [1024, 128], replicated, may hold values from -3 to 3
Outputs:
- alignment_output: float32 [512, 768, 256], P('row', 'col')
- pair_increment: float32 [768, 768, 128], P('row', 'col')
All inputs are finite; a program needn't handle non-finite values.
Results may differ from a plain program's by a relative error of at most 0.0095.
Values may be sent and summed in bfloat16 or wider, within the bound.
No kernel may reach another device: no remote copies, remote signals or barrier semaphores. Data moves between devices by JAX's collectives and lax.ppermute only.
A program may use at most 128 MiB of HBM per device.

v0:
```python
import functools

import jax
import jax.numpy as jnp
import numpy as np
from jax import lax
from jax.experimental import pallas as pl
from jax.experimental.pallas import tpu as pltpu
from jax.sharding import PartitionSpec as P


HEADS = 8
HEAD_DIM = 32
ROWS = 8
COLS = 32
SEQ = 64
RES = 24
OWN = RES // ROWS
TOTAL = SEQ * ROWS
PAIR_ROWS = RES * COLS // ROWS
BLOCK = OWN * SEQ
GROUP = 4
SIDE = OWN * 32
QUARTER = 4 * SIDE
MIB = 1 << 20
C = 256
COPM = 32
CZ = 128
EPS = 1e-05
BF = jnp.bfloat16
F32 = jnp.float32
VMEM = pl.BlockSpec(memory_space=pltpu.VMEM)
SMEM = pl.BlockSpec(memory_space=pltpu.SMEM)
ANY = pl.BlockSpec(memory_space=pl.ANY)


def dot(a, b):
    return jnp.dot(a, b, preferred_element_type=F32)


def iota(shape, dim):
    return lax.broadcasted_iota(jnp.int32, shape, dim)


def column(values):
    return jnp.broadcast_to(values, (8, values.shape[1])).T[:, 0:1]


def norm_kernel(place_ref, align_ref, gain_ref, *refs):
    outs, halves = refs[:ROWS], refs[ROWS:]
    for i in range(2):
        halves[i][...] = align_ref[:, i * 128 : (i + 1) * 128]
    rank = place_ref[0]
    gain = gain_ref[...]
    row = iota((SEQ, 128), 0)
    lane = iota((SEQ, 128), 1)
    row16 = iota((16, 128), 0)
    for n in range(ROWS):
        first = lax.rem(rank + n, ROWS) * OWN
        extra = jnp.zeros((16, 128), F32)
        for j in range(OWN):
            x = jnp.concatenate([half[pl.ds(first + j, SEQ, stride=RES), :] for half in halves], 1)
            centred = x - jnp.mean(x, -1, keepdims=True)
            spread = jnp.mean(centred * centred, -1, keepdims=True) + EPS
            normed = centred * lax.rsqrt(spread) * gain
            outs[n][j * SEQ : (j + 1) * SEQ, :] = normed.astype(BF)
            sigma = jnp.sqrt(spread)
            high = sigma.astype(BF).astype(F32)
            low = sigma - high
            spots = jnp.where(lane == row, high, jnp.where(lane == row + SEQ, low, 0.0))
            extra = extra + jnp.where(row16 == j, jnp.sum(spots, 0, keepdims=True), 0.0)
        outs[n][BLOCK : BLOCK + 16, 0:128] = extra.astype(BF)
        outs[n][BLOCK : BLOCK + 16, 128:256] = jnp.zeros((16, 128), BF)


def attend_kernel(*refs):
    place_ref, res_mask_ref = refs[:2]
    blocks = refs[2:10]
    (wq_ref, wk_ref, wv_ref, wg_ref, wo_ref, gain_ref, gain2_ref, wl_ref, wr_ref, mask_ref) = refs[10:20]
    back_ref, left_ref, rights_ref, gated_ref, gate_ref = refs[20:]
    rank = place_ref[0]
    first_res = place_ref[1] * RES + rank * OWN
    seen = jnp.broadcast_to(mask_ref[...].astype(F32), (8, TOTAL))
    seen = pltpu.roll(seen, lax.rem(ROWS - rank, ROWS) * SEQ, 1)[0:1]
    bias = column(jnp.where(seen > 0, 0.0, -1000000000.0))
    inv_gain = column(1.0 / gain_ref[...])
    gain2 = column(gain2_ref[...])
    wq, wv, wg, wo = (ref[...].T for ref in (wq_ref, wv_ref, wg_ref, wo_ref))
    wlr = jnp.concatenate([wl_ref[...].astype(F32), wr_ref[...].astype(F32)], 1).T.astype(BF)
    lane_head = iota((1, C), 1) // HEAD_DIM
    half = iota((1, 128), 1) < SEQ
    for j in range(OWN):
        x = jnp.concatenate([b[j * SEQ : (j + 1) * SEQ, :] for b in blocks], 0)
        xt = x.T
        keys = dot(x, wk_ref[...]).astype(BF)
        qt = (dot(wq, xt) * HEAD_DIM**-0.5).astype(BF)
        vt = dot(wv, xt).astype(BF)
        gate_ref[...] = jax.nn.sigmoid(dot(wg, xt))
        for h in range(HEADS):
            own = slice(h * HEAD_DIM, (h + 1) * HEAD_DIM)
            head_keys = keys * (lane_head == h).astype(BF)
            for s in range(TOTAL // C):
                cols = slice(s * C, (s + 1) * C)
                logits = dot(head_keys, qt[:, cols]) + bias
                top = jnp.max(logits, 0, keepdims=True)
                weights = jnp.exp(logits - top)
                total = jnp.sum(weights, 0, keepdims=True)
                mixed = dot(vt[own, :], weights.astype(BF)) / total
                gated_ref[own, cols] = (mixed * gate_ref[own, cols]).astype(BF)
        gated = gated_ref[...]
        rows = gated.T
        for p in range(ROWS):
            back_ref[lax.rem(rank + p, ROWS), j * SEQ : (j + 1) * SEQ, :] = rows[p * SEQ : (p + 1) * SEQ, :]
        pieces = []
        for p in range(0, ROWS, 2):
            tiles = []
            for b in blocks[p : p + 2]:
                tile = b[BLOCK : BLOCK + 16, 0:128].astype(F32)[j : j + 1]
                tiles.append(tile + pltpu.roll(tile, SEQ, 1))
            pieces.append(jnp.where(half, tiles[0], tiles[1]))
        sigma = jnp.concatenate(pieces, 1)
        y = dot(wo, gated) + xt.astype(F32) * inv_gain * sigma
        centred = y - jnp.mean(y, 0, keepdims=True)
        spread = jnp.mean(centred * centred, 0, keepdims=True)
        second = (centred * lax.rsqrt(spread + EPS) * gain2).astype(BF)
        live = res_mask_ref[first_res + j].astype(F32)
        sides = dot(wlr, second) * (seen * live)
        sides = pltpu.roll(sides, rank * SEQ, 1).astype(BF)
        left_ref[j * COPM : (j + 1) * COPM, :] = sides[:COPM]
        for p in range(ROWS):
            rights_ref[p, j * COPM : (j + 1) * COPM, :] = sides[COPM:]


def add_kernel(align_ref, wo_ref, back_ref, out_ref, *halves):
    for n in range(ROWS):
        delta = dot(back_ref[n], wo_ref[...])
        for j in range(OWN):
            for i in range(2):
                part = delta[j * SEQ : (j + 1) * SEQ, i * 128 : (i + 1) * 128]
                halves[i][pl.ds(n * OWN + j, SEQ, stride=RES), :] = part
    for i in range(2):
        lanes = slice(i * 128, (i + 1) * 128)
        out_ref[:, lanes] = align_ref[:, lanes] + halves[i][...]


def widen_kernel(w_ref, out_ref, wide_ref):
    wide_ref[...] = w_ref[...].astype(F32)
    out_ref[...] = jnp.zeros(out_ref.shape, BF)
    for b in range(COPM):
        part = wide_ref[pl.ds(b, COPM, stride=COPM), :].astype(BF)
        for i in range(GROUP):
            start = b * GROUP * COPM + i * COPM
            out_ref[start : start + COPM, i * CZ : (i + 1) * CZ] = part


def order_kernel(order_ref, rights_ref, out_ref):
    pick = (order_ref[...] == iota((RES * COPM, RES * COPM), 1)).astype(BF)
    out_ref[...] = dot(pick, rights_ref[...]).astype(BF)


def pair_kernel(quarters, place_ref, res_mask_ref, mask_ref, wide_ref, right_ref, *refs):
    count = len(quarters)
    lefts = refs[:count]
    out_ref, left_ref, mid_ref, done_ref, in_sems, out_sems = refs[-6:]
    gathers = [
        pltpu.make_async_copy(left, left_ref.at[n * QUARTER : (n + 1) * QUARTER, :], in_sems.at[n])
        for n, left in enumerate(lefts)
    ]
    for copy in gathers:
        copy.start()
    row, col = place_ref[0], place_ref[1]
    total = jnp.sum(mask_ref[...].astype(F32), 1, keepdims=True)
    lines = iota((RES, CZ), 0)
    live = jnp.zeros((RES, CZ), F32)
    for j in range(RES):
        live = jnp.where(lines == j, res_mask_ref[col * RES + j].astype(F32), live)
    inverse = 1.0 / jnp.maximum(total * live, 1.0)
    depth, across = col // 8, lax.rem(col // 2, 4)
    residues = []
    for shifted, other in quarters:
        side = lax.rem(col + other, 2)
        place_x = lax.rem(across + 8 - shifted - 2 * lax.rem(row, 2), 4)
        far = lax.rem(place_x + 1, 4) // 2
        for n in range(4):
            source = place_x // 2 * 4 + lax.rem(depth + 4 - n, 4)
            residues.append((2 * far + side) * RES + source * OWN)
    for copy in gathers:
        copy.wait()
    for t in range(count * QUARTER // C):
        block = lax.dot_general(
            right_ref[...], left_ref[t * C : (t + 1) * C, :], (((1,), (1,)), ((), ())), preferred_element_type=F32
        )
        for b in range(COPM):
            rows = block[b * RES : (b + 1) * RES]
            mid_ref[t * 2 * RES : (t + 1) * 2 * RES, b * 128 : (b + 1) * 128] = jnp.concatenate(
                [rows[:, :128], rows[:, 128:]], 0
            ).astype(BF)
    for half in range(2):
        block = dot(mid_ref[...], wide_ref[:, half * C : (half + 1) * C])
        for t in range(len(residues) * OWN // GROUP):
            for i in range(2):
                res = t * GROUP + half * 2 + i
                known = res_mask_ref[row * PAIR_ROWS + residues[res // OWN] + res % OWN]
                scale = jnp.where(known > 0, inverse, 1.0)
                done_ref[res] = block[t * RES : (t + 1) * RES, i * CZ : (i + 1) * CZ] * scale
    copies = [
        pltpu.make_async_copy(
            done_ref.at[n * OWN : (n + 1) * OWN], out_ref.at[pl.ds(residues[n], OWN)], out_sems.at[n]
        )
        for n in range(len(residues))
    ]
    for copy in copies:
        copy.start()
    for copy in copies:
        copy.wait()


def shift(n):
    return [(d, (d + n) % ROWS) for d in range(ROWS)]


def shift_x(n):
    return [(c, c // 8 * 8 + (c + 2 * n) % 8) for c in range(COLS)]


SWAP = [(c, c ^ 1) for c in range(COLS)]


def scatter(depth):
    pairs = []
    for r in range(ROWS):
        for c in range(COLS):
            block, far, core = c // 4, c // 2 % 2, c % 2
            across = (2 * (block % 2) + far + (r // 4 if far else -(r // 4))) % 4
            pairs.append((r * COLS + c, block * COLS + (r + depth) % 4 * 8 + across * 2 + core))
    return pairs


ORDER = np.array(
    [[j // OWN * SIDE + j % OWN * COPM + b] for b in range(COPM) for j in range(RES)], np.int32
)


def shards(
    alignment,
    seq_mask,
    res_mask,
    attn_gain,
    outer_product_gain,
    w_query,
    w_key,
    w_value,
    w_gate,
    output_weight,
    w_left,
    w_right,
    w_pair,
):
    place = jnp.stack([lax.axis_index("row"), lax.axis_index("col")]).astype(jnp.int32)
    tokens = alignment.reshape(SEQ * RES, C)
    mask = seq_mask[None]
    sent = pl.pallas_call(
        norm_kernel,
        out_shape=[jax.ShapeDtypeStruct((BLOCK + 16, C), BF)] * ROWS,
        in_specs=[SMEM, VMEM, VMEM],
        out_specs=[VMEM] * ROWS,
        scratch_shapes=[pltpu.VMEM((SEQ * RES, 128), F32)] * 2,
        compiler_params=pltpu.CompilerParams(vmem_limit_bytes=16 * MIB),
        name="norm",
    )(place, tokens, attn_gain[None])
    blocks = [sent[0]] + [None] * (ROWS - 1)
    for n in FIRST:
        blocks[ROWS - n] = lax.ppermute(sent[n], "row", shift(n))

    wide = pl.pallas_call(
        widen_kernel,
        out_shape=jax.ShapeDtypeStruct((COPM * GROUP * COPM, GROUP * CZ), BF),
        in_specs=[VMEM],
        out_specs=VMEM,
        scratch_shapes=[pltpu.VMEM((COPM * COPM, CZ), F32)],
        compiler_params=pltpu.CompilerParams(vmem_limit_bytes=16 * MIB),
        name="widen",
    )(w_pair)
    back, left, rights = pl.pallas_call(
        attend_kernel,
        out_shape=[
            jax.ShapeDtypeStruct((ROWS, BLOCK, C), BF),
            jax.ShapeDtypeStruct((SIDE, TOTAL), BF),
            jax.ShapeDtypeStruct((ROWS, SIDE, TOTAL), BF),
        ],
        in_specs=[SMEM] * 2 + [VMEM] * 18,
        out_specs=[VMEM] * 3,
        scratch_shapes=[pltpu.VMEM((C, TOTAL), BF), pltpu.VMEM((C, TOTAL), F32)],
        compiler_params=pltpu.CompilerParams(vmem_limit_bytes=24 * MIB),
        name="attend",
    )(
        place,
        res_mask,
        *blocks,
        w_query,
        w_key,
        w_value,
        w_gate,
        output_weight,
        attn_gain[None],
        outer_product_gain[None],
        w_left,
        w_right,
        mask,
    )

    rights = exchanged(rights)
    along_z = [lax.ppermute(left, ("row", "col"), scatter(n)) for n in range(4)]
    own = {0: jnp.concatenate(along_z, 0)}
    for m in (1, 3, 2):
        own[m] = lax.ppermute(own[0], "col", shift_x(m))
    other = {m: lax.ppermute(own[m], "col", SWAP) for m in range(4)}
    back = exchanged(back)
    right_all = pl.pallas_call(
        order_kernel,
        out_shape=jax.ShapeDtypeStruct((RES * COPM, TOTAL), BF),
        in_specs=[VMEM] * 2,
        out_specs=VMEM,
        compiler_params=pltpu.CompilerParams(vmem_limit_bytes=16 * MIB),
        name="order",
    )(ORDER, rights.reshape(RES * COPM, TOTAL))
    pair = []
    for moves in ((0, 1, 3), (2,)):
        quarters = [(m, side) for m in moves for side in range(2)]
        count = len(quarters)
        pair = [
            pl.pallas_call(
                functools.partial(pair_kernel, quarters),
                out_shape=jax.ShapeDtypeStruct((PAIR_ROWS, RES, CZ), F32),
                in_specs=[SMEM] * 2 + [VMEM] * 3 + [ANY] * (count + len(pair)),
                out_specs=ANY,
                scratch_shapes=[
                    pltpu.VMEM((count * QUARTER, TOTAL), BF),
                    pltpu.VMEM((count * 3 * RES, COPM * GROUP * COPM), BF),
                    pltpu.VMEM((count * 4 * OWN, RES, CZ), F32),
                    pltpu.SemaphoreType.DMA((count,)),
                    pltpu.SemaphoreType.DMA((count * 4,)),
                ],
                input_output_aliases={5 + count: 0} if pair else {},
                compiler_params=pltpu.CompilerParams(vmem_limit_bytes=28 * MIB),
            )(place, res_mask, mask, wide, right_all, *((own, other)[side][m] for m, side in quarters), *pair)
        ]
    added = pl.pallas_call(
        add_kernel,
        out_shape=jax.ShapeDtypeStruct((SEQ * RES, C), F32),
        in_specs=[VMEM] * 3,
        out_specs=VMEM,
        scratch_shapes=[pltpu.VMEM((SEQ * RES, 128), F32)] * 2,
        compiler_params=pltpu.CompilerParams(vmem_limit_bytes=16 * MIB),
        name="add",
    )(tokens, output_weight, back)
    return added.reshape(SEQ, RES, C), pair[0]


FIRST = (1, 7, 3, 5, 4, 2, 6)


def exchanged(values):
    return lax.all_to_all(values, "row", split_axis=0, concat_axis=0, tiled=True)


def solution(mesh):
    in_specs = (P("row", "col", None),) + (P(),) * 12
    out_specs = (P("row", "col", None), P("row", "col", None))

    def step(*args):
        return shards(*args)

    step = jax.shard_map(step, mesh=mesh, in_specs=in_specs, out_specs=out_specs, check_vma=False)
    return step
```

profile of v0, /device:TPU:41, one launch (start us, length us, event | category | flops | bytes accessed | tf_op | source)
XLA Modules:
  0.0 138.0 jit_solution(3188669095516639488)
XLA Ops:
  2.9 2.4 %norm.1 = (bf16[208,256]{1,0:T(8,128)(2,1)S(1)}, bf16[208,256]{1,0:T(8,128)(2,1)S(1)}, bf16[208,256]{1,0:T(8,128)(2,1)S(1)}, bf16[208,256]{1,0:T(8,128)(2,1)S(1)...) custom-call(s32[2]{0:T(128)S(1)} %pad_add_fusion.place_ref.refs_0_, ...), custom_call_target="tpu_custom_call" | custom-call | tf_op jit(solution)/shard_map/norm/pallas_call | solution.py:262
  5.5 1.9 %collective-permute-start.1 = (bf16[208,256]{1,0:T(8,128)(2,1)S(1)}, bf16[208,256]{1,0:T(8,128)(2,1)S(1)}, u32[]{:S(2)}, u32[]{:S(2)}) collective-permute-start(bf16[208,256]{1,0:T(8,128)(2,1)S(1)} %get-tuple-element.15), channel_id=1, source_target_pairs={{0,192},{32,224},{64,0},{96,32},{128,64},{160,96},{192,128},{224,1... | collective-permute-start | bytes 319496 | tf_op jit(solution)/shard_map/ppermute | solution.py:273
  7.4 3.0 %collective-permute-start.2 = (bf16[208,256]{1,0:T(8,128)(2,1)S(1)}, bf16[208,256]{1,0:T(8,128)(2,1)S(1)}, u32[]{:S(2)}, u32[]{:S(2)}) collective-permute-start(bf16[208,256]{1,0:T(8,128)(2,1)S(1)} %get-tuple-element.16), channel_id=1, source_target_pairs={{0,160},{32,192},{64,224},{96,0},{128,32},{160,64},{192,96},{224,1... | collective-permute-start | bytes 319496 | tf_op jit(solution)/shard_map/ppermute | solution.py:273
  11.4 2.0 %collective-permute-start.5 = (bf16[208,256]{1,0:T(8,128)(2,1)S(1)}, bf16[208,256]{1,0:T(8,128)(2,1)S(1)}, u32[]{:S(2)}, u32[]{:S(2)}) collective-permute-start(bf16[208,256]{1,0:T(8,128)(2,1)S(1)} %get-tuple-element.19), channel_id=1, source_target_pairs={{0,64},{32,96},{64,128},{96,160},{128,192},{160,224},{192,0},{224,... | collective-permute-start | bytes 319496 | tf_op jit(solution)/shard_map/ppermute | solution.py:273
  13.4 1.6 %collective-permute-start.6 = (bf16[208,256]{1,0:T(8,128)(2,1)S(1)}, bf16[208,256]{1,0:T(8,128)(2,1)S(1)}, u32[]{:S(2)}, u32[]{:S(2)}) collective-permute-start(bf16[208,256]{1,0:T(8,128)(2,1)S(1)} %get-tuple-element.20), channel_id=1, source_target_pairs={{0,32},{32,64},{64,96},{96,128},{128,160},{160,192},{192,224},{224... | collective-permute-start | bytes 319496 | tf_op jit(solution)/shard_map/ppermute | solution.py:273
  18.4 2.1 %collective-permute-done.6.refs_9_ = bf16[208,256]{1,0:T(8,128)(2,1)S(1)} collective-permute-done((bf16[208,256]{1,0:T(8,128)(2,1)S(1)}, bf16[208,256]{1,0:T(8,128)(2,1)S(1)}, u32[]{:S(2)}, u32[]{:S(2)}) %collective-permute-start.6) | collective-permute-done | bytes 106528 | tf_op jit(solution)/shard_map/ppermute | solution.py:273
  20.6 23.2 %attend.1 = (bf16[8,192,256]{2,1,0:T(8,128)(2,1)}, bf16[96,512]{1,0:T(8,128)(2,1)S(1)}, bf16[8,96,512]{2,1,0:T(8,128)(2,1)S(1)}) custom-call(s32[2]{0:T(128)S(1)} %pad_add_fusion.place_ref.refs_0_, s32[768]{0:T(1024)S(1)} %copy-done.12, bf16[208,256]{1,0:T(8,128)(2,1)S(1)} %get-tuple-element.13.refs_2_, bf16[208,256]{1,0:T(8,128)(2,1)S(1)} %collective-permute-done.refs_3_, ...), custom_call_target="tpu_custom_call" | custom-call | tf_op jit(solution)/shard_map/attend/pallas_call | solution.py:284
  43.7 14.8 %all_to_all.10 = bf16[8,96,512]{2,1,0:T(8,128)(2,1)S(1)} all-to-all(bf16[8,96,512]{2,1,0:T(8,128)(2,1)S(1)} %get-tuple-element.22), channel_id=1, replica_groups=mesh['row'=8,'col'=32] {'row'}, dimensions={0} | all-to-all | bytes 1572864 | tf_op jit(solution)/shard_map/all_to_all | solution.py:364
  58.6 4.4 %all-to-all-start = ((bf16[8,192,256]{2,1,0:T(8,128)(2,1)}), bf16[8,192,256]{2,1,0:T(8,128)(2,1)}, u32[]{:S(2)}, u32[]{:S(2)}) async-start(bf16[8,192,256]{2,1,0:T(8,128)(2,1)} %get-tuple-element.21), calls=%async_computation | async-start | bytes 1572864 | tf_op jit(solution)/shard_map/all_to_all | solution.py:364
  62.9 6.4 %collective-permute-start.7 = (bf16[96,512]{1,0:T(8,128)(2,1)S(1)}, bf16[96,512]{1,0:T(8,128)(2,1)S(1)}, u32[]{:S(2)}, u32[]{:S(2)}) collective-permute-start(bf16[96,512]{1,0:T(8,128)(2,1)S(1)} %get-tuple-element.23), channel_id=1, source_target_pairs={{0,0},{1,1},{2,2},{3,3},{4,36},{5,37},{6,38},{7,39},{8,64},{9,65},... | collective-permute-start | bytes 294920 | tf_op jit(solution)/shard_map/ppermute | solution.py:313
  69.3 3.8 %collective-permute-start.8 = (bf16[96,512]{1,0:T(8,128)(2,1)S(1)}, bf16[96,512]{1,0:T(8,128)(2,1)S(1)}, u32[]{:S(2)}, u32[]{:S(2)}) collective-permute-start(bf16[96,512]{1,0:T(8,128)(2,1)S(1)} %get-tuple-element.23), channel_id=1, source_target_pairs={{0,8},{1,9},{2,10},{3,11},{4,44},{5,45},{6,46},{7,47},{8,72},{9,73... | collective-permute-start | bytes 294920 | tf_op jit(solution)/shard_map/ppermute | solution.py:313
  73.1 8.6 %collective-permute-start.9 = (bf16[96,512]{1,0:T(8,128)(2,1)S(1)}, bf16[96,512]{1,0:T(8,128)(2,1)S(1)}, u32[]{:S(2)}, u32[]{:S(2)}) collective-permute-start(bf16[96,512]{1,0:T(8,128)(2,1)S(1)} %get-tuple-element.23), channel_id=1, source_target_pairs={{0,16},{1,17},{2,18},{3,19},{4,52},{5,53},{6,54},{7,55},{8,80},{9,... | collective-permute-start | bytes 294920 | tf_op jit(solution)/shard_map/ppermute | solution.py:313
  81.7 1.9 %collective-permute-start.10 = (bf16[96,512]{1,0:T(8,128)(2,1)S(1)}, bf16[96,512]{1,0:T(8,128)(2,1)S(1)}, u32[]{:S(2)}, u32[]{:S(2)}) collective-permute-start(bf16[96,512]{1,0:T(8,128)(2,1)S(1)} %get-tuple-element.23), channel_id=1, source_target_pairs={{0,24},{1,25},{2,26},{3,27},{4,60},{5,61},{6,62},{7,63},{8,88},{9,... | collective-permute-start | bytes 294920 | tf_op jit(solution)/shard_map/ppermute | solution.py:313
  83.7 2.0 %collective-permute-done.9 = bf16[96,512]{1,0:T(8,128)(2,1)S(1)} collective-permute-done((bf16[96,512]{1,0:T(8,128)(2,1)S(1)}, bf16[96,512]{1,0:T(8,128)(2,1)S(1)}, u32[]{:S(2)}, u32[]{:S(2)}) %collective-permute-start.9) | collective-permute-done | bytes 98336 | tf_op jit(solution)/shard_map/ppermute | solution.py:313
  85.7 7.6 %collective-permute-done.10 = bf16[96,512]{1,0:T(8,128)(2,1)S(1)} collective-permute-done((bf16[96,512]{1,0:T(8,128)(2,1)S(1)}, bf16[96,512]{1,0:T(8,128)(2,1)S(1)}, u32[]{:S(2)}, u32[]{:S(2)}) %collective-permute-start.10) | collective-permute-done | bytes 98336 | tf_op jit(solution)/shard_map/ppermute | solution.py:313
  93.5 2.7 %collective-permute-start.16 = (bf16[384,512]{1,0:T(8,128)(2,1)S(1)}, bf16[384,512]{1,0:T(8,128)(2,1)}, u32[]{:S(2)}, u32[]{:S(2)}) collective-permute-start(bf16[384,512]{1,0:T(8,128)(2,1)S(1)} %constant_dynamic-update-slice_fusion.refs_0_), channel_id=1, source_target_pairs={{0,6},{1,7},{2,0},{3,1},{4,2},{5,3},{6,4},{7,5},{8,14},{9,15},{10,... | collective-permute-start | bytes 1179656 | tf_op jit(solution)/shard_map/ppermute | solution.py:316
  96.1 6.3 %collective-permute-start.13 = (bf16[384,512]{1,0:T(8,128)(2,1)S(1)}, bf16[384,512]{1,0:T(8,128)(2,1)}, u32[]{:S(2)}, u32[]{:S(2)}) collective-permute-start(bf16[384,512]{1,0:T(8,128)(2,1)S(1)} %constant_dynamic-update-slice_fusion.refs_0_), channel_id=1, source_target_pairs={{0,1},{1,0},{2,3},{3,2},{4,5},{5,4},{6,7},{7,6},{8,9},{9,8},{10,11... | collective-permute-start | bytes 1179656 | tf_op jit(solution)/shard_map/ppermute | solution.py:317
  102.4 9.5 %collective-permute-done.14.refs_2_ = bf16[384,512]{1,0:T(8,128)(2,1)} collective-permute-done((bf16[384,512]{1,0:T(8,128)(2,1)S(1)}, bf16[384,512]{1,0:T(8,128)(2,1)}, u32[]{:S(2)}, u32[]{:S(2)}) %collective-permute-start.14) | collective-permute-done | bytes 393248 | tf_op jit(solution)/shard_map/ppermute | solution.py:316
  111.9 3.9 %collective-permute-start.15 = (bf16[384,512]{1,0:T(8,128)(2,1)}, bf16[384,512]{1,0:T(8,128)(2,1)}, u32[]{:S(2)}, u32[]{:S(2)}) collective-permute-start(bf16[384,512]{1,0:T(8,128)(2,1)} %collective-permute-done.14.refs_2_), channel_id=1, source_target_pairs={{0,1},{1,0},{2,3},{3,2},{4,5},{5,4},{6,7},{7,6},{8,9},{9,8},{10,11... | collective-permute-start | bytes 1179656 | tf_op jit(solution)/shard_map/ppermute | solution.py:317
  117.0 2.0 %copy-done = bf16[4096,512]{1,0:T(8,128)(2,1)} copy-done((bf16[4096,512]{1,0:T(8,128)(2,1)}, bf16[4096,512]{1,0:T(8,128)(2,1)S(1)}, u32[]{:S(2)}) %copy-start) | copy-done | bytes 4194328
  121.3 2.9 %add.3 = f32[1536,256]{1,0:T(8,128)} custom-call(f32[1536,256]{1,0:T(8,128)S(1)} %bitcast.9, bf16[256,256]{1,0:T(8,128)(2,1)S(1)} %copy-done.5, bf16[8,192,256]{2,1,0:T(8,128)(2,1)} %all-to-all-done.back_ref), custom_call_target="tpu_custom_call" | custom-call | tf_op jit(solution)/shard_map/add/pallas_call | solution.py:348
  124.2 2.2 %copy-done.1 = bf16[4096,512]{1,0:T(8,128)(2,1)S(1)} copy-done((bf16[4096,512]{1,0:T(8,128)(2,1)S(1)}, bf16[4096,512]{1,0:T(8,128)(2,1)}, u32[]{:S(2)}) %copy-start.1) | copy-done | bytes 4194328
  126.4 7.4 %shard_map.149.refs_2_ = f32[96,24,128]{2,1,0:T(8,128)} custom-call(s32[2]{0:T(128)S(1)} %pad_add_fusion.place_ref.refs_0_, s32[768]{0:T(1024)S(1)} %copy-done.12, s32[1,512]{1,0:T(1,128)S(1)} %bitcast.12, bf16[4096,512]{1,0:T(8,128)(2,1)S(1)} %copy-done.1, bf16[768,512]{1,0:T(8,128)(2,1)S(1)} %order.1.right_ref, ...), custom_call_target="tpu_custom_call" | custom-call | tf_op jit(solution)/shard_map/pallas_call | solution.py:332
  133.8 4.0 %shard_map.150 = f32[96,24,128]{2,1,0:T(8,128)} custom-call(s32[2]{0:T(128)S(1)} %pad_add_fusion.place_ref.refs_0_, s32[768]{0:T(1024)S(1)} %copy-done.12, s32[1,512]{1,0:T(1,128)S(1)} %bitcast.13, bf16[4096,512]{1,0:T(8,128)(2,1)S(1)} %copy-done.1, bf16[768,512]{1,0:T(8,128)(2,1)S(1)} %order.1.right_ref, ...), custom_call_target="tpu_custom_call", output_to_operand_aliasing={{}: (7, {})} | custom-call | tf_op jit(solution)/shard_map/pallas_call | solution.py:332
  (67 shorter events, 10.5 us)
Async XLA Ops:
  0.6 19.9 %copy-start.15 = (f32[256]{0:T(256)S(1)}, f32[256]{0:T(256)}, u32[]{:S(2)}) copy-start(f32[256]{0:T(256)} %param.17) | copy-start | bytes 3076
  0.6 19.9 %copy-start.13 = (s32[512]{0:T(512)S(1)}, s32[512]{0:T(512)}, u32[]{:S(2)}) copy-start(s32[512]{0:T(512)} %param.15) | copy-start | bytes 6148
  0.7 19.9 %copy-start.16 = (f32[256]{0:T(256)S(1)}, f32[256]{0:T(256)}, u32[]{:S(2)}) copy-start(f32[256]{0:T(256)} %param.18) | copy-start | bytes 3076
  5.3 6.1 %collective-permute-start = (bf16[208,256]{1,0:T(8,128)(2,1)S(1)}, bf16[208,256]{1,0:T(8,128)(2,1)S(1)}, u32[]{:S(2)}, u32[]{:S(2)}) collective-permute-start(bf16[208,256]{1,0:T(8,128)(2,1)S(1)} %get-tuple-element.14), channel_id=1, source_target_pairs={{0,224},{32,0},{64,32},{96,64},{128,96},{160,128},{192,160},{224,1... | collective-permute-start | bytes 319496 | tf_op jit(solution)/shard_map/ppermute | solution.py:273
  5.5 7.9 %collective-permute-start.1 = (bf16[208,256]{1,0:T(8,128)(2,1)S(1)}, bf16[208,256]{1,0:T(8,128)(2,1)S(1)}, u32[]{:S(2)}, u32[]{:S(2)}) collective-permute-start(bf16[208,256]{1,0:T(8,128)(2,1)S(1)} %get-tuple-element.15), channel_id=1, source_target_pairs={{0,192},{32,224},{64,0},{96,32},{128,64},{160,96},{192,128},{224,1... | collective-permute-start | bytes 319496 | tf_op jit(solution)/shard_map/ppermute | solution.py:273
  7.4 8.7 %collective-permute-start.2 = (bf16[208,256]{1,0:T(8,128)(2,1)S(1)}, bf16[208,256]{1,0:T(8,128)(2,1)S(1)}, u32[]{:S(2)}, u32[]{:S(2)}) collective-permute-start(bf16[208,256]{1,0:T(8,128)(2,1)S(1)} %get-tuple-element.16), channel_id=1, source_target_pairs={{0,160},{32,192},{64,224},{96,0},{128,32},{160,64},{192,96},{224,1... | collective-permute-start | bytes 319496 | tf_op jit(solution)/shard_map/ppermute | solution.py:273
  10.3 5.8 %collective-permute-start.3 = (bf16[208,256]{1,0:T(8,128)(2,1)S(1)}, bf16[208,256]{1,0:T(8,128)(2,1)S(1)}, u32[]{:S(2)}, u32[]{:S(2)}) collective-permute-start(bf16[208,256]{1,0:T(8,128)(2,1)S(1)} %get-tuple-element.17), channel_id=1, source_target_pairs={{0,128},{32,160},{64,192},{96,224},{128,0},{160,32},{192,64},{224,... | collective-permute-start | bytes 319496 | tf_op jit(solution)/shard_map/ppermute | solution.py:273
  10.3 6.7 %collective-permute-start.4 = (bf16[208,256]{1,0:T(8,128)(2,1)S(1)}, bf16[208,256]{1,0:T(8,128)(2,1)S(1)}, u32[]{:S(2)}, u32[]{:S(2)}) collective-permute-start(bf16[208,256]{1,0:T(8,128)(2,1)S(1)} %get-tuple-element.18), channel_id=1, source_target_pairs={{0,96},{32,128},{64,160},{96,192},{128,224},{160,0},{192,32},{224,... | collective-permute-start | bytes 319496 | tf_op jit(solution)/shard_map/ppermute | solution.py:273
  11.4 7.0 %collective-permute-start.5 = (bf16[208,256]{1,0:T(8,128)(2,1)S(1)}, bf16[208,256]{1,0:T(8,128)(2,1)S(1)}, u32[]{:S(2)}, u32[]{:S(2)}) collective-permute-start(bf16[208,256]{1,0:T(8,128)(2,1)S(1)} %get-tuple-element.19), channel_id=1, source_target_pairs={{0,64},{32,96},{64,128},{96,160},{128,192},{160,224},{192,0},{224,... | collective-permute-start | bytes 319496 | tf_op jit(solution)/shard_map/ppermute | solution.py:273
  13.4 7.1 %collective-permute-start.6 = (bf16[208,256]{1,0:T(8,128)(2,1)S(1)}, bf16[208,256]{1,0:T(8,128)(2,1)S(1)}, u32[]{:S(2)}, u32[]{:S(2)}) collective-permute-start(bf16[208,256]{1,0:T(8,128)(2,1)S(1)} %get-tuple-element.20), channel_id=1, source_target_pairs={{0,32},{32,64},{64,96},{96,128},{128,160},{160,192},{192,224},{224... | collective-permute-start | bytes 319496 | tf_op jit(solution)/shard_map/ppermute | solution.py:273
  58.6 57.7 %copy-start.7 = (bf16[1024,128]{1,0:T(8,128)(2,1)S(1)}, bf16[1024,128]{1,0:T(8,128)(2,1)}, u32[]{:S(2)}) copy-start(bf16[1024,128]{1,0:T(8,128)(2,1)} %w_ref.1) | copy-start | bytes 786436
  58.6 61.2 %all-to-all-start = ((bf16[8,192,256]{2,1,0:T(8,128)(2,1)}), bf16[8,192,256]{2,1,0:T(8,128)(2,1)}, u32[]{:S(2)}, u32[]{:S(2)}) async-start(bf16[8,192,256]{2,1,0:T(8,128)(2,1)} %get-tuple-element.21), calls=%async_computation | async-start | bytes 1572864 | tf_op jit(solution)/shard_map/all_to_all | solution.py:364
  62.9 20.7 %collective-permute-start.7 = (bf16[96,512]{1,0:T(8,128)(2,1)S(1)}, bf16[96,512]{1,0:T(8,128)(2,1)S(1)}, u32[]{:S(2)}, u32[]{:S(2)}) collective-permute-start(bf16[96,512]{1,0:T(8,128)(2,1)S(1)} %get-tuple-element.23), channel_id=1, source_target_pairs={{0,0},{1,1},{2,2},{3,3},{4,36},{5,37},{6,38},{7,39},{8,64},{9,65},... | collective-permute-start | bytes 294920 | tf_op jit(solution)/shard_map/ppermute | solution.py:313
  69.3 14.4 %collective-permute-start.8 = (bf16[96,512]{1,0:T(8,128)(2,1)S(1)}, bf16[96,512]{1,0:T(8,128)(2,1)S(1)}, u32[]{:S(2)}, u32[]{:S(2)}) collective-permute-start(bf16[96,512]{1,0:T(8,128)(2,1)S(1)} %get-tuple-element.23), channel_id=1, source_target_pairs={{0,8},{1,9},{2,10},{3,11},{4,44},{5,45},{6,46},{7,47},{8,72},{9,73... | collective-permute-start | bytes 294920 | tf_op jit(solution)/shard_map/ppermute | solution.py:313
  73.1 12.6 %collective-permute-start.9 = (bf16[96,512]{1,0:T(8,128)(2,1)S(1)}, bf16[96,512]{1,0:T(8,128)(2,1)S(1)}, u32[]{:S(2)}, u32[]{:S(2)}) collective-permute-start(bf16[96,512]{1,0:T(8,128)(2,1)S(1)} %get-tuple-element.23), channel_id=1, source_target_pairs={{0,16},{1,17},{2,18},{3,19},{4,52},{5,53},{6,54},{7,55},{8,80},{9,... | collective-permute-start | bytes 294920 | tf_op jit(solution)/shard_map/ppermute | solution.py:313
  81.7 11.6 %collective-permute-start.10 = (bf16[96,512]{1,0:T(8,128)(2,1)S(1)}, bf16[96,512]{1,0:T(8,128)(2,1)S(1)}, u32[]{:S(2)}, u32[]{:S(2)}) collective-permute-start(bf16[96,512]{1,0:T(8,128)(2,1)S(1)} %get-tuple-element.23), channel_id=1, source_target_pairs={{0,24},{1,25},{2,26},{3,27},{4,60},{5,61},{6,62},{7,63},{8,88},{9,... | collective-permute-start | bytes 294920 | tf_op jit(solution)/shard_map/ppermute | solution.py:313
  93.4 25.6 %copy-start.6 = (s32[768,1]{1,0:T(8,128)S(1)}, s32[768,1]{1,0:T(8,128)}, u32[]{:S(2)}) copy-start(s32[768,1]{1,0:T(8,128)} %constant.11.clone.order_ref) | copy-start | bytes 9220
  93.4 18.5 %collective-permute-start.14 = (bf16[384,512]{1,0:T(8,128)(2,1)S(1)}, bf16[384,512]{1,0:T(8,128)(2,1)}, u32[]{:S(2)}, u32[]{:S(2)}) collective-permute-start(bf16[384,512]{1,0:T(8,128)(2,1)S(1)} %constant_dynamic-update-slice_fusion.refs_0_), channel_id=1, source_target_pairs={{0,2},{1,3},{2,4},{3,5},{4,6},{5,7},{6,0},{7,1},{8,10},{9,11},{10,... | collective-permute-start | bytes 1179656 | tf_op jit(solution)/shard_map/ppermute | solution.py:316
  93.5 22.3 %collective-permute-start.16 = (bf16[384,512]{1,0:T(8,128)(2,1)S(1)}, bf16[384,512]{1,0:T(8,128)(2,1)}, u32[]{:S(2)}, u32[]{:S(2)}) collective-permute-start(bf16[384,512]{1,0:T(8,128)(2,1)S(1)} %constant_dynamic-update-slice_fusion.refs_0_), channel_id=1, source_target_pairs={{0,6},{1,7},{2,0},{3,1},{4,2},{5,3},{6,4},{7,5},{8,14},{9,15},{10,... | collective-permute-start | bytes 1179656 | tf_op jit(solution)/shard_map/ppermute | solution.py:316
  96.1 19.7 %collective-permute-start.11 = (bf16[384,512]{1,0:T(8,128)(2,1)S(1)}, bf16[384,512]{1,0:T(8,128)(2,1)}, u32[]{:S(2)}, u32[]{:S(2)}) collective-permute-start(bf16[384,512]{1,0:T(8,128)(2,1)S(1)} %constant_dynamic-update-slice_fusion.refs_0_), channel_id=1, source_target_pairs={{0,4},{1,5},{2,6},{3,7},{4,0},{5,1},{6,2},{7,3},{8,12},{9,13},{10,... | collective-permute-start | bytes 1179656 | tf_op jit(solution)/shard_map/ppermute | solution.py:316
  96.1 28.0 %collective-permute-start.13 = (bf16[384,512]{1,0:T(8,128)(2,1)S(1)}, bf16[384,512]{1,0:T(8,128)(2,1)}, u32[]{:S(2)}, u32[]{:S(2)}) collective-permute-start(bf16[384,512]{1,0:T(8,128)(2,1)S(1)} %constant_dynamic-update-slice_fusion.refs_0_), channel_id=1, source_target_pairs={{0,1},{1,0},{2,3},{3,2},{4,5},{5,4},{6,7},{7,6},{8,9},{9,8},{10,11... | collective-permute-start | bytes 1179656 | tf_op jit(solution)/shard_map/ppermute | solution.py:317
  111.9 12.3 %collective-permute-start.15 = (bf16[384,512]{1,0:T(8,128)(2,1)}, bf16[384,512]{1,0:T(8,128)(2,1)}, u32[]{:S(2)}, u32[]{:S(2)}) collective-permute-start(bf16[384,512]{1,0:T(8,128)(2,1)} %collective-permute-done.14.refs_2_), channel_id=1, source_target_pairs={{0,1},{1,0},{2,3},{3,2},{4,5},{5,4},{6,7},{7,6},{8,9},{9,8},{10,11... | collective-permute-start | bytes 1179656 | tf_op jit(solution)/shard_map/ppermute | solution.py:317
  115.8 8.4 %collective-permute-start.17 = (bf16[384,512]{1,0:T(8,128)(2,1)}, bf16[384,512]{1,0:T(8,128)(2,1)}, u32[]{:S(2)}, u32[]{:S(2)}) collective-permute-start(bf16[384,512]{1,0:T(8,128)(2,1)} %collective-permute-done.16.refs_4_), channel_id=1, source_target_pairs={{0,1},{1,0},{2,3},{3,2},{4,5},{5,4},{6,7},{7,6},{8,9},{9,8},{10,11... | collective-permute-start | bytes 1179656 | tf_op jit(solution)/shard_map/ppermute | solution.py:317
  115.8 18.0 %collective-permute-start.12 = (bf16[384,512]{1,0:T(8,128)(2,1)}, bf16[384,512]{1,0:T(8,128)(2,1)}, u32[]{:S(2)}, u32[]{:S(2)}) collective-permute-start(bf16[384,512]{1,0:T(8,128)(2,1)} %collective-permute-done.11.refs_0_), channel_id=1, source_target_pairs={{0,1},{1,0},{2,3},{3,2},{4,5},{5,4},{6,7},{7,6},{8,9},{9,8},{10,11... | collective-permute-start | bytes 1179656 | tf_op jit(solution)/shard_map/ppermute | solution.py:317
  (14 other events, 141.3 us)
where the time goes:
time: 138 us
  starting transfers between devices  48.2 us (35%)
  Pallas kernels  41.3 us (30%)
  waiting for transfers between devices  24.4 us (18%)
  blocking collectives  14.8 us (11%)
  local copies, waits for them, and re-layouts  8.05 us (6%)
    pallas_call x1, Pallas kernels, shards(): pl.pallas_call(attend_kernel, out_shape=[jax.ShapeDtypeStruct((ROWS, BLOC...  23.2 us
    ppermute x4, starting transfers between devices, shards(): along_z = [lax.ppermute(left, ('row', 'col'), scatter(n)) for n in range(4)]  20.7 us
    all_to_all x1, blocking collectives, exchanged(): lax.all_to_all(values, 'row', split_axis=0, concat_axis=0, tiled=True)  14.8 us
    pallas_call x2, Pallas kernels, shards(): pl.pallas_call(functools.partial(pair_kernel, quarters), out_shape=jax.Sh...  11.4 us
    ppermute x4, starting transfers between devices, shards(): other = {m: lax.ppermute(own[m], 'col', SWAP) for m in range(4)}  10.7 us
    ppermute x7, starting transfers between devices, shards(): blocks[ROWS - n] = lax.ppermute(sent[n], 'row', shift(n))  9.73 us
    ppermute x4, waiting for transfers between devices, shards(): along_z = [lax.ppermute(left, ('row', 'col'), scatter(n)) for n in range(4)]  9.64 us
    ppermute x3, waiting for transfers between devices, shards(): own[m] = lax.ppermute(own[0], 'col', shift_x(m))  9.47 us
  transfers between devices with their start and end apart: 19, of which 7 were waited for; matrix products, arithmetic and copies ran while one was open for 0% of the time, Pallas kernels for 9%

commit v1 on v0

--- a/solution.py
+++ b/solution.py
@@ -9,7 +9,6 @@
 from jax.sharding import PartitionSpec as P
 
 
-HEADS = 8
 HEAD_DIM = 32
 ROWS = 8
 COLS = 32
@@ -77,40 +76,43 @@
     place_ref, res_mask_ref = refs[:2]
     blocks = refs[2:10]
     (wq_ref, wk_ref, wv_ref, wg_ref, wo_ref, gain_ref, gain2_ref, wl_ref, wr_ref, mask_ref) = refs[10:20]
-    back_ref, left_ref, rights_ref, gated_ref, gate_ref = refs[20:]
+    out_ref, left_ref, gated_ref, gate_ref = refs[20:]
     rank = place_ref[0]
     first_res = place_ref[1] * RES + rank * OWN
     seen = jnp.broadcast_to(mask_ref[...].astype(F32), (8, TOTAL))
     seen = pltpu.roll(seen, lax.rem(ROWS - rank, ROWS) * SEQ, 1)[0:1]
-    bias = column(jnp.where(seen > 0, 0.0, -1000000000.0))
+    bias = jnp.where(seen > 0, 0.0, -1000000000.0)
     inv_gain = column(1.0 / gain_ref[...])
     gain2 = column(gain2_ref[...])
-    wq, wv, wg, wo = (ref[...].T for ref in (wq_ref, wv_ref, wg_ref, wo_ref))
+    wk, wo = wk_ref[...].T, wo_ref[...].T
     wlr = jnp.concatenate([wl_ref[...].astype(F32), wr_ref[...].astype(F32)], 1).T.astype(BF)
     lane_head = iota((1, C), 1) // HEAD_DIM
     half = iota((1, 128), 1) < SEQ
+    tile_head = iota((TOTAL, 128), 1) // HEAD_DIM
+    ones = jnp.ones((TOTAL, 128), BF)
     for j in range(OWN):
         x = jnp.concatenate([b[j * SEQ : (j + 1) * SEQ, :] for b in blocks], 0)
         xt = x.T
-        keys = dot(x, wk_ref[...]).astype(BF)
-        qt = (dot(wq, xt) * HEAD_DIM**-0.5).astype(BF)
-        vt = dot(wv, xt).astype(BF)
-        gate_ref[...] = jax.nn.sigmoid(dot(wg, xt))
-        for h in range(HEADS):
-            own = slice(h * HEAD_DIM, (h + 1) * HEAD_DIM)
-            head_keys = keys * (lane_head == h).astype(BF)
-            for s in range(TOTAL // C):
-                cols = slice(s * C, (s + 1) * C)
-                logits = dot(head_keys, qt[:, cols]) + bias
-                top = jnp.max(logits, 0, keepdims=True)
-                weights = jnp.exp(logits - top)
-                total = jnp.sum(weights, 0, keepdims=True)
-                mixed = dot(vt[own, :], weights.astype(BF)) / total
-                gated_ref[own, cols] = (mixed * gate_ref[own, cols]).astype(BF)
-        gated = gated_ref[...]
-        rows = gated.T
+        queries = (dot(x, wq_ref[...]) * HEAD_DIM**-0.5).astype(BF)
+        kt = dot(wk, xt).astype(BF)
+        values = dot(x, wv_ref[...]).astype(BF)
+        gate_ref[...] = jax.nn.sigmoid(dot(x, wg_ref[...]))
+        for tile in range(C // 128):
+            lanes = slice(tile * 128, (tile + 1) * 128)
+            wide = jnp.concatenate([values[:, lanes], ones], 1)
+            mixed = jnp.zeros((TOTAL, 128), F32)
+            for h in range(128 // HEAD_DIM):
+                picked = (lane_head == tile * (128 // HEAD_DIM) + h).astype(BF)
+                logits = dot(queries * picked, kt) + bias
+                top = jnp.max(logits, 1, keepdims=True)
+                weights = jnp.exp(logits - top).astype(BF)
+                both = dot(weights, wide)
+                mixed = jnp.where(tile_head == h, both[:, :128] / both[:, 128:], mixed)
+            gated_ref[:, lanes] = (mixed * gate_ref[:, lanes]).astype(BF)
+        rows = gated_ref[...]
+        gated = rows.T
         for p in range(ROWS):
-            back_ref[lax.rem(rank + p, ROWS), j * SEQ : (j + 1) * SEQ, :] = rows[p * SEQ : (p + 1) * SEQ, :]
+            out_ref[lax.rem(rank + p, ROWS), j * SEQ : (j + 1) * SEQ, :] = rows[p * SEQ : (p + 1) * SEQ, :]
         pieces = []
         for p in range(0, ROWS, 2):
             tiles = []
@@ -128,12 +130,14 @@
         sides = pltpu.roll(sides, rank * SEQ, 1).astype(BF)
         left_ref[j * COPM : (j + 1) * COPM, :] = sides[:COPM]
         for p in range(ROWS):
-            rights_ref[p, j * COPM : (j + 1) * COPM, :] = sides[COPM:]
-
-
-def add_kernel(align_ref, wo_ref, back_ref, out_ref, *halves):
+            for i in range(2):
+                spot = BLOCK + i * SIDE + j * COPM
+                out_ref[p, spot : spot + COPM, :] = sides[COPM:, i * C : (i + 1) * C]
+
+
+def add_kernel(align_ref, wo_ref, mixed_ref, out_ref, *halves):
     for n in range(ROWS):
-        delta = dot(back_ref[n], wo_ref[...])
+        delta = dot(mixed_ref[n, 0:BLOCK, :], wo_ref[...])
         for j in range(OWN):
             for i in range(2):
                 part = delta[j * SEQ : (j + 1) * SEQ, i * 128 : (i + 1) * 128]
@@ -153,9 +157,12 @@
             out_ref[start : start + COPM, i * CZ : (i + 1) * CZ] = part
 
 
-def order_kernel(order_ref, rights_ref, out_ref):
+def order_kernel(order_ref, mixed_ref, out_ref):
     pick = (order_ref[...] == iota((RES * COPM, RES * COPM), 1)).astype(BF)
-    out_ref[...] = dot(pick, rights_ref[...]).astype(BF)
+    for i in range(2):
+        start = BLOCK + i * SIDE
+        part = jnp.concatenate([mixed_ref[n, start : start + SIDE, :] for n in range(ROWS)], 0)
+        out_ref[:, i * C : (i + 1) * C] = dot(pick, part).astype(BF)
 
 
 def pair_kernel(quarters, place_ref, res_mask_ref, mask_ref, wide_ref, right_ref, *refs):
@@ -281,17 +288,16 @@
         compiler_params=pltpu.CompilerParams(vmem_limit_bytes=16 * MIB),
         name="widen",
     )(w_pair)
-    back, left, rights = pl.pallas_call(
+    mixed, left = pl.pallas_call(
         attend_kernel,
         out_shape=[
-            jax.ShapeDtypeStruct((ROWS, BLOCK, C), BF),
+            jax.ShapeDtypeStruct((ROWS, BLOCK + 2 * SIDE, C), BF),
             jax.ShapeDtypeStruct((SIDE, TOTAL), BF),
-            jax.ShapeDtypeStruct((ROWS, SIDE, TOTAL), BF),
         ],
         in_specs=[SMEM] * 2 + [VMEM] * 18,
-        out_specs=[VMEM] * 3,
-        scratch_shapes=[pltpu.VMEM((C, TOTAL), BF), pltpu.VMEM((C, TOTAL), F32)],
-        compiler_params=pltpu.CompilerParams(vmem_limit_bytes=24 * MIB),
+        out_specs=[VMEM] * 2,
+        scratch_shapes=[pltpu.VMEM((TOTAL, C), BF), pltpu.VMEM((TOTAL, C), F32)],
+        compiler_params=pltpu.CompilerParams(vmem_limit_bytes=16 * MIB),
         name="attend",
     )(
         place,
@@ -309,13 +315,12 @@
         mask,
     )
 
-    rights = exchanged(rights)
+    mixed = exchanged(mixed)
     along_z = [lax.ppermute(left, ("row", "col"), scatter(n)) for n in range(4)]
     own = {0: jnp.concatenate(along_z, 0)}
     for m in (1, 3, 2):
         own[m] = lax.ppermute(own[0], "col", shift_x(m))
     other = {m: lax.ppermute(own[m], "col", SWAP) for m in range(4)}
-    back = exchanged(back)
     right_all = pl.pallas_call(
         order_kernel,
         out_shape=jax.ShapeDtypeStruct((RES * COPM, TOTAL), BF),
@@ -323,7 +328,7 @@
         out_specs=VMEM,
         compiler_params=pltpu.CompilerParams(vmem_limit_bytes=16 * MIB),
         name="order",
-    )(ORDER, rights.reshape(RES * COPM, TOTAL))
+    )(ORDER, mixed)
     pair = []
     for moves in ((0, 1, 3), (2,)):
         quarters = [(m, side) for m in moves for side in range(2)]
@@ -353,7 +358,7 @@
         scratch_shapes=[pltpu.VMEM((SEQ * RES, 128), F32)] * 2,
         compiler_params=pltpu.CompilerParams(vmem_limit_bytes=16 * MIB),
         name="add",
-    )(tokens, output_weight, back)
+    )(tokens, output_weight, mixed)
     return added.reshape(SEQ, RES, C), pair[0]
 
 

time: 138 us -> 113 us (0.82)
  blocking collectives: 14.8 us -> 0 us
  Pallas kernels: 41.3 us -> 29.1 us
  waiting for transfers between devices: 24.4 us -> 27.8 us
  local copies, waits for them, and re-layouts: 8.05 us -> 6.54 us
    all_to_all x1 -> x0, blocking collectives: 14.8 us -> none  [exchanged(): lax.all_to_all(values, 'row', split_axis=0, concat_axis=0, tiled=True)]
    pallas_call x1, Pallas kernels: 23.2 us -> 12.1 us  [shards(): pl.pallas_call(attend_kernel, out_shape=[jax.ShapeDtypeStruct((ROWS, BLOC...]
    ppermute x4, waiting for transfers between devices: 9.64 us -> 12.3 us  [shards(): along_z = [lax.ppermute(left, ('row', 'col'), scatter(n)) for n in range(4)]]
    ppermute x4, starting transfers between devices: 10.7 us -> 8.92 us  [shards(): other = {m: lax.ppermute(own[m], 'col', SWAP) for m in range(4)}]
    all_to_all x1, starting transfers between devices: 4.37 us -> 5.96 us  [exchanged(): lax.all_to_all(values, 'row', split_axis=0, concat_axis=0, tiled=True)]
    unnamed x43, local copies, waits for them, and re-layouts: 8.04 us -> 6.53 us
  transfers between devices with their start and end apart: 19 -> 19, of which waited for: 7 -> 9; matrix products, arithmetic and copies ran while one was open for 0% -> 0% of each run, Pallas kernels for 9% -> 9%
where the time goes in v1:
time: 113 us
  starting transfers between devices  48.2 us (43%)
  Pallas kernels  29.1 us (26%)
  waiting for transfers between devices  27.8 us (25%)
  local copies, waits for them, and re-layouts  6.54 us (6%)
    ppermute x4, starting transfers between devices, shards(): along_z = [lax.ppermute(left, ('row', 'col'), scatter(n)) for n in range(4)]  20.6 us
    ppermute x4, waiting for transfers between devices, shards(): along_z = [lax.ppermute(left, ('row', 'col'), scatter(n)) for n in range(4)]  12.3 us
    pallas_call x1, Pallas kernels, shards(): pl.pallas_call(attend_kernel, out_shape=[jax.ShapeDtypeStruct((ROWS, BLOC...  12.1 us
    pallas_call x2, Pallas kernels, shards(): pl.pallas_call(functools.partial(pair_kernel, quarters), out_shape=jax.Sh...  11.4 us
    ppermute x3, waiting for transfers between devices, shards(): own[m] = lax.ppermute(own[0], 'col', shift_x(m))  10.2 us
    ppermute x7, starting transfers between devices, shards(): blocks[ROWS - n] = lax.ppermute(sent[n], 'row', shift(n))  9.73 us
    ppermute x4, starting transfers between devices, shards(): other = {m: lax.ppermute(own[m], 'col', SWAP) for m in range(4)}  8.92 us
    unnamed x43, local copies, waits for them, and re-layouts  6.53 us
  transfers between devices with their start and end apart: 19, of which 9 were waited for; matrix products, arithmetic and copies ran while one was open for 0% of the time, Pallas kernels for 9%

profile of v1, /device:TPU:41, one launch (start us, length us, event | category | flops | bytes accessed | tf_op | source)
XLA Modules:
  0.0 112.7 jit_solution(12611122116693761512)
XLA Ops:
  0.8 1.4 %copy-done.2 = f32[64,24,256]{2,1,0:T(8,128)S(1)} copy-done((f32[64,24,256]{2,1,0:T(8,128)S(1)}, f32[64,24,256]{2,1,0:T(8,128)}, u32[]{:S(2)}) %copy-start.2) | copy-done | bytes 1572888
  2.9 2.4 %norm.1 = (bf16[208,256]{1,0:T(8,128)(2,1)S(1)}, bf16[208,256]{1,0:T(8,128)(2,1)S(1)}, bf16[208,256]{1,0:T(8,128)(2,1)S(1)}, bf16[208,256]{1,0:T(8,128)(2,1)S(1)...) custom-call(s32[2]{0:T(128)S(1)} %pad_add_fusion.place_ref.refs_0_, ...), custom_call_target="tpu_custom_call" | custom-call | tf_op jit(solution)/shard_map/norm/pallas_call | solution.py:269
  5.5 1.9 %collective-permute-start.1 = (bf16[208,256]{1,0:T(8,128)(2,1)S(1)}, bf16[208,256]{1,0:T(8,128)(2,1)S(1)}, u32[]{:S(2)}, u32[]{:S(2)}) collective-permute-start(bf16[208,256]{1,0:T(8,128)(2,1)S(1)} %get-tuple-element.14), channel_id=1, source_target_pairs={{0,192},{32,224},{64,0},{96,32},{128,64},{160,96},{192,128},{224,1... | collective-permute-start | bytes 319496 | tf_op jit(solution)/shard_map/ppermute | solution.py:280
  7.4 3.0 %collective-permute-start.2 = (bf16[208,256]{1,0:T(8,128)(2,1)S(1)}, bf16[208,256]{1,0:T(8,128)(2,1)S(1)}, u32[]{:S(2)}, u32[]{:S(2)}) collective-permute-start(bf16[208,256]{1,0:T(8,128)(2,1)S(1)} %get-tuple-element.15), channel_id=1, source_target_pairs={{0,160},{32,192},{64,224},{96,0},{128,32},{160,64},{192,96},{224,1... | collective-permute-start | bytes 319496 | tf_op jit(solution)/shard_map/ppermute | solution.py:280
  11.4 2.0 %collective-permute-start.5 = (bf16[208,256]{1,0:T(8,128)(2,1)S(1)}, bf16[208,256]{1,0:T(8,128)(2,1)S(1)}, u32[]{:S(2)}, u32[]{:S(2)}) collective-permute-start(bf16[208,256]{1,0:T(8,128)(2,1)S(1)} %get-tuple-element.18), channel_id=1, source_target_pairs={{0,64},{32,96},{64,128},{96,160},{128,192},{160,224},{192,0},{224,... | collective-permute-start | bytes 319496 | tf_op jit(solution)/shard_map/ppermute | solution.py:280
  13.4 1.6 %collective-permute-start.6 = (bf16[208,256]{1,0:T(8,128)(2,1)S(1)}, bf16[208,256]{1,0:T(8,128)(2,1)S(1)}, u32[]{:S(2)}, u32[]{:S(2)}) collective-permute-start(bf16[208,256]{1,0:T(8,128)(2,1)S(1)} %get-tuple-element.19), channel_id=1, source_target_pairs={{0,32},{32,64},{64,96},{96,128},{128,160},{160,192},{192,224},{224... | collective-permute-start | bytes 319496 | tf_op jit(solution)/shard_map/ppermute | solution.py:280
  17.0 1.3 %collective-permute-done.5.refs_8_ = bf16[208,256]{1,0:T(8,128)(2,1)S(1)} collective-permute-done((bf16[208,256]{1,0:T(8,128)(2,1)S(1)}, bf16[208,256]{1,0:T(8,128)(2,1)S(1)}, u32[]{:S(2)}, u32[]{:S(2)}) %collective-permute-start.5) | collective-permute-done | bytes 106528 | tf_op jit(solution)/shard_map/ppermute | solution.py:280
  18.4 2.1 %collective-permute-done.6.refs_9_ = bf16[208,256]{1,0:T(8,128)(2,1)S(1)} collective-permute-done((bf16[208,256]{1,0:T(8,128)(2,1)S(1)}, bf16[208,256]{1,0:T(8,128)(2,1)S(1)}, u32[]{:S(2)}, u32[]{:S(2)}) %collective-permute-start.6) | collective-permute-done | bytes 106528 | tf_op jit(solution)/shard_map/ppermute | solution.py:280
  20.6 12.1 %attend.1 = (bf16[8,384,256]{2,1,0:T(8,128)(2,1)}, bf16[96,512]{1,0:T(8,128)(2,1)S(1)}) custom-call(s32[2]{0:T(128)S(1)} %pad_add_fusion.place_ref.refs_0_, s32[768]{0:T(1024)S(1)} %copy-done.12, bf16[208,256]{1,0:T(8,128)(2,1)S(1)} %get-tuple-element.12.refs_2_, bf16[208,256]{1,0:T(8,128)(2,1)S(1)} %collective-permute-done.refs_3_, ...), custom_call_target="tpu_custom_call" | custom-call | tf_op jit(solution)/shard_map/attend/pallas_call | solution.py:291
  32.7 6.0 %all-to-all-start = ((bf16[8,384,256]{2,1,0:T(8,128)(2,1)}), bf16[8,384,256]{2,1,0:T(8,128)(2,1)S(1)}, u32[]{:S(2)}, u32[]{:S(2)}) async-start(bf16[8,384,256]{2,1,0:T(8,128)(2,1)} %get-tuple-element.20), calls=%async_computation | async-start | bytes 3145728 | tf_op jit(solution)/shard_map/all_to_all | solution.py:369
  38.6 6.2 %collective-permute-start.7 = (bf16[96,512]{1,0:T(8,128)(2,1)S(1)}, bf16[96,512]{1,0:T(8,128)(2,1)S(1)}, u32[]{:S(2)}, u32[]{:S(2)}) collective-permute-start(bf16[96,512]{1,0:T(8,128)(2,1)S(1)} %get-tuple-element.21), channel_id=1, source_target_pairs={{0,0},{1,1},{2,2},{3,3},{4,36},{5,37},{6,38},{7,39},{8,64},{9,65},... | collective-permute-start | bytes 294920 | tf_op jit(solution)/shard_map/ppermute | solution.py:319
  44.9 3.8 %collective-permute-start.8 = (bf16[96,512]{1,0:T(8,128)(2,1)S(1)}, bf16[96,512]{1,0:T(8,128)(2,1)S(1)}, u32[]{:S(2)}, u32[]{:S(2)}) collective-permute-start(bf16[96,512]{1,0:T(8,128)(2,1)S(1)} %get-tuple-element.21), channel_id=1, source_target_pairs={{0,8},{1,9},{2,10},{3,11},{4,44},{5,45},{6,46},{7,47},{8,72},{9,73... | collective-permute-start | bytes 294920 | tf_op jit(solution)/shard_map/ppermute | solution.py:319
  48.7 8.6 %collective-permute-start.9 = (bf16[96,512]{1,0:T(8,128)(2,1)S(1)}, bf16[96,512]{1,0:T(8,128)(2,1)S(1)}, u32[]{:S(2)}, u32[]{:S(2)}) collective-permute-start(bf16[96,512]{1,0:T(8,128)(2,1)S(1)} %get-tuple-element.21), channel_id=1, source_target_pairs={{0,16},{1,17},{2,18},{3,19},{4,52},{5,53},{6,54},{7,55},{8,80},{9,... | collective-permute-start | bytes 294920 | tf_op jit(solution)/shard_map/ppermute | solution.py:319
  57.3 1.9 %collective-permute-start.10 = (bf16[96,512]{1,0:T(8,128)(2,1)S(1)}, bf16[96,512]{1,0:T(8,128)(2,1)S(1)}, u32[]{:S(2)}, u32[]{:S(2)}) collective-permute-start(bf16[96,512]{1,0:T(8,128)(2,1)S(1)} %get-tuple-element.21), channel_id=1, source_target_pairs={{0,24},{1,25},{2,26},{3,27},{4,60},{5,61},{6,62},{7,63},{8,88},{9,... | collective-permute-start | bytes 294920 | tf_op jit(solution)/shard_map/ppermute | solution.py:319
  59.3 9.7 %collective-permute-done.7 = bf16[96,512]{1,0:T(8,128)(2,1)S(1)} collective-permute-done((bf16[96,512]{1,0:T(8,128)(2,1)S(1)}, bf16[96,512]{1,0:T(8,128)(2,1)S(1)}, u32[]{:S(2)}, u32[]{:S(2)}) %collective-permute-start.7) | collective-permute-done | bytes 98336 | tf_op jit(solution)/shard_map/ppermute | solution.py:319
  69.4 1.4 %collective-permute-done.9 = bf16[96,512]{1,0:T(8,128)(2,1)S(1)} collective-permute-done((bf16[96,512]{1,0:T(8,128)(2,1)S(1)}, bf16[96,512]{1,0:T(8,128)(2,1)S(1)}, u32[]{:S(2)}, u32[]{:S(2)}) %collective-permute-start.9) | collective-permute-done | bytes 98336 | tf_op jit(solution)/shard_map/ppermute | solution.py:319
  71.9 2.7 %collective-permute-start.16 = (bf16[384,512]{1,0:T(8,128)(2,1)S(1)}, bf16[384,512]{1,0:T(8,128)(2,1)}, u32[]{:S(2)}, u32[]{:S(2)}) collective-permute-start(bf16[384,512]{1,0:T(8,128)(2,1)S(1)} %constant_dynamic-update-slice_fusion.refs_0_), channel_id=1, source_target_pairs={{0,6},{1,7},{2,0},{3,1},{4,2},{5,3},{6,4},{7,5},{8,14},{9,15},{10,... | collective-permute-start | bytes 1179656 | tf_op jit(solution)/shard_map/ppermute | solution.py:322
  74.6 4.9 %collective-permute-start.13 = (bf16[384,512]{1,0:T(8,128)(2,1)S(1)}, bf16[384,512]{1,0:T(8,128)(2,1)}, u32[]{:S(2)}, u32[]{:S(2)}) collective-permute-start(bf16[384,512]{1,0:T(8,128)(2,1)S(1)} %constant_dynamic-update-slice_fusion.refs_0_), channel_id=1, source_target_pairs={{0,1},{1,0},{2,3},{3,2},{4,5},{5,4},{6,7},{7,6},{8,9},{9,8},{10,11... | collective-permute-start | bytes 1179656 | tf_op jit(solution)/shard_map/ppermute | solution.py:323
  79.6 10.2 %collective-permute-done.14.refs_2_ = bf16[384,512]{1,0:T(8,128)(2,1)} collective-permute-done((bf16[384,512]{1,0:T(8,128)(2,1)S(1)}, bf16[384,512]{1,0:T(8,128)(2,1)}, u32[]{:S(2)}, u32[]{:S(2)}) %collective-permute-start.14) | collective-permute-done | bytes 393248 | tf_op jit(solution)/shard_map/ppermute | solution.py:322
  89.7 3.5 %collective-permute-start.15 = (bf16[384,512]{1,0:T(8,128)(2,1)}, bf16[384,512]{1,0:T(8,128)(2,1)}, u32[]{:S(2)}, u32[]{:S(2)}) collective-permute-start(bf16[384,512]{1,0:T(8,128)(2,1)} %collective-permute-done.14.refs_2_), channel_id=1, source_target_pairs={{0,1},{1,0},{2,3},{3,2},{4,5},{5,4},{6,7},{7,6},{8,9},{9,8},{10,11... | collective-permute-start | bytes 1179656 | tf_op jit(solution)/shard_map/ppermute | solution.py:323
  95.4 2.0 %copy-done = bf16[4096,512]{1,0:T(8,128)(2,1)} copy-done((bf16[4096,512]{1,0:T(8,128)(2,1)}, bf16[4096,512]{1,0:T(8,128)(2,1)S(1)}, u32[]{:S(2)}) %copy-start) | copy-done | bytes 4194328
  98.3 1.7 %add.3 = f32[1536,256]{1,0:T(8,128)} custom-call(f32[1536,256]{1,0:T(8,128)S(1)} %bitcast.8, bf16[256,256]{1,0:T(8,128)(2,1)S(1)} %copy-done.5, bf16[8,384,256]{2,1,0:T(8,128)(2,1)S(1)} %all-to-all-done.mixed_ref), custom_call_target="tpu_custom_call" | custom-call | tf_op jit(solution)/shard_map/add/pallas_call | solution.py:353
  101.2 7.4 %shard_map.149.refs_2_ = f32[96,24,128]{2,1,0:T(8,128)} custom-call(s32[2]{0:T(128)S(1)} %pad_add_fusion.place_ref.refs_0_, s32[768]{0:T(1024)S(1)} %copy-done.12, s32[1,512]{1,0:T(1,128)S(1)} %bitcast.10, bf16[4096,512]{1,0:T(8,128)(2,1)S(1)} %copy-done.1, bf16[768,512]{1,0:T(8,128)(2,1)S(1)} %order.1.right_ref, ...), custom_call_target="tpu_custom_call" | custom-call | tf_op jit(solution)/shard_map/pallas_call | solution.py:337
  108.6 4.0 %shard_map.150 = f32[96,24,128]{2,1,0:T(8,128)} custom-call(s32[2]{0:T(128)S(1)} %pad_add_fusion.place_ref.refs_0_, s32[768]{0:T(1024)S(1)} %copy-done.12, s32[1,512]{1,0:T(1,128)S(1)} %bitcast.11, bf16[4096,512]{1,0:T(8,128)(2,1)S(1)} %copy-done.1, bf16[768,512]{1,0:T(8,128)(2,1)S(1)} %order.1.right_ref, ...), custom_call_target="tpu_custom_call", output_to_operand_aliasing={{}: (7, {})} | custom-call | tf_op jit(solution)/shard_map/pallas_call | solution.py:337
  (66 shorter events, 9.9 us)
Async XLA Ops:
  0.6 19.9 %copy-start.15 = (f32[256]{0:T(256)S(1)}, f32[256]{0:T(256)}, u32[]{:S(2)}) copy-start(f32[256]{0:T(256)} %param.17) | copy-start | bytes 3076
  0.6 19.9 %copy-start.13 = (s32[512]{0:T(512)S(1)}, s32[512]{0:T(512)}, u32[]{:S(2)}) copy-start(s32[512]{0:T(512)} %param.15) | copy-start | bytes 6148
  0.7 19.9 %copy-start.16 = (f32[256]{0:T(256)S(1)}, f32[256]{0:T(256)}, u32[]{:S(2)}) copy-start(f32[256]{0:T(256)} %param.18) | copy-start | bytes 3076
  0.7 19.8 %copy-start.12 = (s32[768]{0:T(1024)S(1)}, s32[768]{0:T(1024)}, u32[]{:S(2)}) copy-start(s32[768]{0:T(1024)} %res_mask_ref.3) | copy-start | bytes 9220
  5.3 6.1 %collective-permute-start = (bf16[208,256]{1,0:T(8,128)(2,1)S(1)}, bf16[208,256]{1,0:T(8,128)(2,1)S(1)}, u32[]{:S(2)}, u32[]{:S(2)}) collective-permute-start(bf16[208,256]{1,0:T(8,128)(2,1)S(1)} %get-tuple-element.13), channel_id=1, source_target_pairs={{0,224},{32,0},{64,32},{96,64},{128,96},{160,128},{192,160},{224,1... | collective-permute-start | bytes 319496 | tf_op jit(solution)/shard_map/ppermute | solution.py:280
  5.5 7.9 %collective-permute-start.1 = (bf16[208,256]{1,0:T(8,128)(2,1)S(1)}, bf16[208,256]{1,0:T(8,128)(2,1)S(1)}, u32[]{:S(2)}, u32[]{:S(2)}) collective-permute-start(bf16[208,256]{1,0:T(8,128)(2,1)S(1)} %get-tuple-element.14), channel_id=1, source_target_pairs={{0,192},{32,224},{64,0},{96,32},{128,64},{160,96},{192,128},{224,1... | collective-permute-start | bytes 319496 | tf_op jit(solution)/shard_map/ppermute | solution.py:280
  7.4 8.7 %collective-permute-start.2 = (bf16[208,256]{1,0:T(8,128)(2,1)S(1)}, bf16[208,256]{1,0:T(8,128)(2,1)S(1)}, u32[]{:S(2)}, u32[]{:S(2)}) collective-permute-start(bf16[208,256]{1,0:T(8,128)(2,1)S(1)} %get-tuple-element.15), channel_id=1, source_target_pairs={{0,160},{32,192},{64,224},{96,0},{128,32},{160,64},{192,96},{224,1... | collective-permute-start | bytes 319496 | tf_op jit(solution)/shard_map/ppermute | solution.py:280
  10.3 5.8 %collective-permute-start.3 = (bf16[208,256]{1,0:T(8,128)(2,1)S(1)}, bf16[208,256]{1,0:T(8,128)(2,1)S(1)}, u32[]{:S(2)}, u32[]{:S(2)}) collective-permute-start(bf16[208,256]{1,0:T(8,128)(2,1)S(1)} %get-tuple-element.16), channel_id=1, source_target_pairs={{0,128},{32,160},{64,192},{96,224},{128,0},{160,32},{192,64},{224,... | collective-permute-start | bytes 319496 | tf_op jit(solution)/shard_map/ppermute | solution.py:280
  10.3 6.7 %collective-permute-start.4 = (bf16[208,256]{1,0:T(8,128)(2,1)S(1)}, bf16[208,256]{1,0:T(8,128)(2,1)S(1)}, u32[]{:S(2)}, u32[]{:S(2)}) collective-permute-start(bf16[208,256]{1,0:T(8,128)(2,1)S(1)} %get-tuple-element.17), channel_id=1, source_target_pairs={{0,96},{32,128},{64,160},{96,192},{128,224},{160,0},{192,32},{224,... | collective-permute-start | bytes 319496 | tf_op jit(solution)/shard_map/ppermute | solution.py:280
  11.4 7.0 %collective-permute-start.5 = (bf16[208,256]{1,0:T(8,128)(2,1)S(1)}, bf16[208,256]{1,0:T(8,128)(2,1)S(1)}, u32[]{:S(2)}, u32[]{:S(2)}) collective-permute-start(bf16[208,256]{1,0:T(8,128)(2,1)S(1)} %get-tuple-element.18), channel_id=1, source_target_pairs={{0,64},{32,96},{64,128},{96,160},{128,192},{160,224},{192,0},{224,... | collective-permute-start | bytes 319496 | tf_op jit(solution)/shard_map/ppermute | solution.py:280
  13.4 7.1 %collective-permute-start.6 = (bf16[208,256]{1,0:T(8,128)(2,1)S(1)}, bf16[208,256]{1,0:T(8,128)(2,1)S(1)}, u32[]{:S(2)}, u32[]{:S(2)}) collective-permute-start(bf16[208,256]{1,0:T(8,128)(2,1)S(1)} %get-tuple-element.19), channel_id=1, source_target_pairs={{0,32},{32,64},{64,96},{96,128},{128,160},{160,192},{192,224},{224... | collective-permute-start | bytes 319496 | tf_op jit(solution)/shard_map/ppermute | solution.py:280
  32.7 64.7 %all-to-all-start = ((bf16[8,384,256]{2,1,0:T(8,128)(2,1)}), bf16[8,384,256]{2,1,0:T(8,128)(2,1)S(1)}, u32[]{:S(2)}, u32[]{:S(2)}) async-start(bf16[8,384,256]{2,1,0:T(8,128)(2,1)} %get-tuple-element.20), calls=%async_computation | async-start | bytes 3145728 | tf_op jit(solution)/shard_map/all_to_all | solution.py:369
  38.6 30.3 %collective-permute-start.7 = (bf16[96,512]{1,0:T(8,128)(2,1)S(1)}, bf16[96,512]{1,0:T(8,128)(2,1)S(1)}, u32[]{:S(2)}, u32[]{:S(2)}) collective-permute-start(bf16[96,512]{1,0:T(8,128)(2,1)S(1)} %get-tuple-element.21), channel_id=1, source_target_pairs={{0,0},{1,1},{2,2},{3,3},{4,36},{5,37},{6,38},{7,39},{8,64},{9,65},... | collective-permute-start | bytes 294920 | tf_op jit(solution)/shard_map/ppermute | solution.py:319
  44.9 24.5 %collective-permute-start.8 = (bf16[96,512]{1,0:T(8,128)(2,1)S(1)}, bf16[96,512]{1,0:T(8,128)(2,1)S(1)}, u32[]{:S(2)}, u32[]{:S(2)}) collective-permute-start(bf16[96,512]{1,0:T(8,128)(2,1)S(1)} %get-tuple-element.21), channel_id=1, source_target_pairs={{0,8},{1,9},{2,10},{3,11},{4,44},{5,45},{6,46},{7,47},{8,72},{9,73... | collective-permute-start | bytes 294920 | tf_op jit(solution)/shard_map/ppermute | solution.py:319
  48.7 22.1 %collective-permute-start.9 = (bf16[96,512]{1,0:T(8,128)(2,1)S(1)}, bf16[96,512]{1,0:T(8,128)(2,1)S(1)}, u32[]{:S(2)}, u32[]{:S(2)}) collective-permute-start(bf16[96,512]{1,0:T(8,128)(2,1)S(1)} %get-tuple-element.21), channel_id=1, source_target_pairs={{0,16},{1,17},{2,18},{3,19},{4,52},{5,53},{6,54},{7,55},{8,80},{9,... | collective-permute-start | bytes 294920 | tf_op jit(solution)/shard_map/ppermute | solution.py:319
  57.3 14.3 %collective-permute-start.10 = (bf16[96,512]{1,0:T(8,128)(2,1)S(1)}, bf16[96,512]{1,0:T(8,128)(2,1)S(1)}, u32[]{:S(2)}, u32[]{:S(2)}) collective-permute-start(bf16[96,512]{1,0:T(8,128)(2,1)S(1)} %get-tuple-element.21), channel_id=1, source_target_pairs={{0,24},{1,25},{2,26},{3,27},{4,60},{5,61},{6,62},{7,63},{8,88},{9,... | collective-permute-start | bytes 294920 | tf_op jit(solution)/shard_map/ppermute | solution.py:319
  71.6 25.8 %copy-start.3 = (f32[64,24,256]{2,1,0:T(8,128)S(1)}, f32[64,24,256]{2,1,0:T(8,128)}, u32[]{:S(2)}) copy-start(f32[64,24,256]{2,1,0:T(8,128)} %param.14) | copy-start | bytes 4718596
  71.6 18.1 %collective-permute-start.14 = (bf16[384,512]{1,0:T(8,128)(2,1)S(1)}, bf16[384,512]{1,0:T(8,128)(2,1)}, u32[]{:S(2)}, u32[]{:S(2)}) collective-permute-start(bf16[384,512]{1,0:T(8,128)(2,1)S(1)} %constant_dynamic-update-slice_fusion.refs_0_), channel_id=1, source_target_pairs={{0,2},{1,3},{2,4},{3,5},{4,6},{5,7},{6,0},{7,1},{8,10},{9,11},{10,... | collective-permute-start | bytes 1179656 | tf_op jit(solution)/shard_map/ppermute | solution.py:322
  71.9 21.3 %collective-permute-start.16 = (bf16[384,512]{1,0:T(8,128)(2,1)S(1)}, bf16[384,512]{1,0:T(8,128)(2,1)}, u32[]{:S(2)}, u32[]{:S(2)}) collective-permute-start(bf16[384,512]{1,0:T(8,128)(2,1)S(1)} %constant_dynamic-update-slice_fusion.refs_0_), channel_id=1, source_target_pairs={{0,6},{1,7},{2,0},{3,1},{4,2},{5,3},{6,4},{7,5},{8,14},{9,15},{10,... | collective-permute-start | bytes 1179656 | tf_op jit(solution)/shard_map/ppermute | solution.py:322
  74.6 18.6 %collective-permute-start.11 = (bf16[384,512]{1,0:T(8,128)(2,1)S(1)}, bf16[384,512]{1,0:T(8,128)(2,1)}, u32[]{:S(2)}, u32[]{:S(2)}) collective-permute-start(bf16[384,512]{1,0:T(8,128)(2,1)S(1)} %constant_dynamic-update-slice_fusion.refs_0_), channel_id=1, source_target_pairs={{0,4},{1,5},{2,6},{3,7},{4,0},{5,1},{6,2},{7,3},{8,12},{9,13},{10,... | collective-permute-start | bytes 1179656 | tf_op jit(solution)/shard_map/ppermute | solution.py:322
  74.6 26.2 %collective-permute-start.13 = (bf16[384,512]{1,0:T(8,128)(2,1)S(1)}, bf16[384,512]{1,0:T(8,128)(2,1)}, u32[]{:S(2)}, u32[]{:S(2)}) collective-permute-start(bf16[384,512]{1,0:T(8,128)(2,1)S(1)} %constant_dynamic-update-slice_fusion.refs_0_), channel_id=1, source_target_pairs={{0,1},{1,0},{2,3},{3,2},{4,5},{5,4},{6,7},{7,6},{8,9},{9,8},{10,11... | collective-permute-start | bytes 1179656 | tf_op jit(solution)/shard_map/ppermute | solution.py:323
  89.7 11.1 %collective-permute-start.15 = (bf16[384,512]{1,0:T(8,128)(2,1)}, bf16[384,512]{1,0:T(8,128)(2,1)}, u32[]{:S(2)}, u32[]{:S(2)}) collective-permute-start(bf16[384,512]{1,0:T(8,128)(2,1)} %collective-permute-done.14.refs_2_), channel_id=1, source_target_pairs={{0,1},{1,0},{2,3},{3,2},{4,5},{5,4},{6,7},{7,6},{8,9},{9,8},{10,11... | collective-permute-start | bytes 1179656 | tf_op jit(solution)/shard_map/ppermute | solution.py:323
  93.2 7.7 %collective-permute-start.17 = (bf16[384,512]{1,0:T(8,128)(2,1)}, bf16[384,512]{1,0:T(8,128)(2,1)}, u32[]{:S(2)}, u32[]{:S(2)}) collective-permute-start(bf16[384,512]{1,0:T(8,128)(2,1)} %collective-permute-done.16.refs_4_), channel_id=1, source_target_pairs={{0,1},{1,0},{2,3},{3,2},{4,5},{5,4},{6,7},{7,6},{8,9},{9,8},{10,11... | collective-permute-start | bytes 1179656 | tf_op jit(solution)/shard_map/ppermute | solution.py:323
  93.2 15.4 %collective-permute-start.12 = (bf16[384,512]{1,0:T(8,128)(2,1)}, bf16[384,512]{1,0:T(8,128)(2,1)}, u32[]{:S(2)}, u32[]{:S(2)}) collective-permute-start(bf16[384,512]{1,0:T(8,128)(2,1)} %collective-permute-done.11.refs_0_), channel_id=1, source_target_pairs={{0,1},{1,0},{2,3},{3,2},{4,5},{5,4},{6,7},{7,6},{8,9},{9,8},{10,11... | collective-permute-start | bytes 1179656 | tf_op jit(solution)/shard_map/ppermute | solution.py:323
  (14 other events, 123.4 us)

commit v2 on v1

--- a/solution.py
+++ b/solution.py
@@ -191,33 +191,41 @@
         for n in range(4):
             source = place_x // 2 * 4 + lax.rem(depth + 4 - n, 4)
             residues.append((2 * far + side) * RES + source * OWN)
-    for copy in gathers:
-        copy.wait()
-    for t in range(count * QUARTER // C):
-        block = lax.dot_general(
-            right_ref[...], left_ref[t * C : (t + 1) * C, :], (((1,), (1,)), ((), ())), preferred_element_type=F32
-        )
-        for b in range(COPM):
-            rows = block[b * RES : (b + 1) * RES]
-            mid_ref[t * 2 * RES : (t + 1) * 2 * RES, b * 128 : (b + 1) * 128] = jnp.concatenate(
-                [rows[:, :128], rows[:, 128:]], 0
-            ).astype(BF)
-    for half in range(2):
-        block = dot(mid_ref[...], wide_ref[:, half * C : (half + 1) * C])
-        for t in range(len(residues) * OWN // GROUP):
-            for i in range(2):
-                res = t * GROUP + half * 2 + i
-                known = res_mask_ref[row * PAIR_ROWS + residues[res // OWN] + res % OWN]
-                scale = jnp.where(known > 0, inverse, 1.0)
-                done_ref[res] = block[t * RES : (t + 1) * RES, i * CZ : (i + 1) * CZ] * scale
-    copies = [
-        pltpu.make_async_copy(
-            done_ref.at[n * OWN : (n + 1) * OWN], out_ref.at[pl.ds(residues[n], OWN)], out_sems.at[n]
-        )
-        for n in range(len(residues))
-    ]
-    for copy in copies:
-        copy.start()
+    landed = 0
+    copies = []
+    tiles = count * QUARTER // C
+    for part in range(2):
+        for t in range(part * tiles // 2, (part + 1) * tiles // 2):
+            while landed * QUARTER < (t + 1) * C:
+                gathers[landed].wait()
+                landed += 1
+            block = lax.dot_general(
+                right_ref[...],
+                left_ref[t * C : (t + 1) * C, :],
+                (((1,), (1,)), ((), ())),
+                preferred_element_type=F32,
+            )
+            for b in range(COPM):
+                rows = block[b * RES : (b + 1) * RES]
+                mid_ref[t * 2 * RES : (t + 1) * 2 * RES, b * 128 : (b + 1) * 128] = jnp.concatenate(
+                    [rows[:, :128], rows[:, 128:]], 0
+                ).astype(BF)
+        groups = range(part * tiles, (part + 1) * tiles)
+        for half in range(2):
+            block = dot(mid_ref[groups[0] * RES : (groups[-1] + 1) * RES, :], wide_ref[:, half * C : (half + 1) * C])
+            for k, t in enumerate(groups):
+                for i in range(2):
+                    res = t * GROUP + half * 2 + i
+                    known = res_mask_ref[row * PAIR_ROWS + residues[res // OWN] + res % OWN]
+                    scale = jnp.where(known > 0, inverse, 1.0)
+                    done_ref[res] = block[k * RES : (k + 1) * RES, i * CZ : (i + 1) * CZ] * scale
+        for n in range(groups[0] * GROUP // OWN, (groups[-1] + 1) * GROUP // OWN):
+            copies.append(
+                pltpu.make_async_copy(
+                    done_ref.at[n * OWN : (n + 1) * OWN], out_ref.at[pl.ds(residues[n], OWN)], out_sems.at[n]
+                )
+            )
+            copies[-1].start()
     for copy in copies:
         copy.wait()
 
@@ -329,27 +337,23 @@
         compiler_params=pltpu.CompilerParams(vmem_limit_bytes=16 * MIB),
         name="order",
     )(ORDER, mixed)
-    pair = []
-    for moves in ((0, 1, 3), (2,)):
-        quarters = [(m, side) for m in moves for side in range(2)]
-        count = len(quarters)
-        pair = [
-            pl.pallas_call(
-                functools.partial(pair_kernel, quarters),
-                out_shape=jax.ShapeDtypeStruct((PAIR_ROWS, RES, CZ), F32),
-                in_specs=[SMEM] * 2 + [VMEM] * 3 + [ANY] * (count + len(pair)),
-                out_specs=ANY,
-                scratch_shapes=[
-                    pltpu.VMEM((count * QUARTER, TOTAL), BF),
-                    pltpu.VMEM((count * 3 * RES, COPM * GROUP * COPM), BF),
-                    pltpu.VMEM((count * 4 * OWN, RES, CZ), F32),
-                    pltpu.SemaphoreType.DMA((count,)),
-                    pltpu.SemaphoreType.DMA((count * 4,)),
-                ],
-                input_output_aliases={5 + count: 0} if pair else {},
-                compiler_params=pltpu.CompilerParams(vmem_limit_bytes=28 * MIB),
-            )(place, res_mask, mask, wide, right_all, *((own, other)[side][m] for m, side in quarters), *pair)
-        ]
+    quarters = [(m, side) for m in (0, 1, 3, 2) for side in range(2)]
+    count = len(quarters)
+    pair = pl.pallas_call(
+        functools.partial(pair_kernel, quarters),
+        out_shape=jax.ShapeDtypeStruct((PAIR_ROWS, RES, CZ), F32),
+        in_specs=[SMEM] * 2 + [VMEM] * 3 + [ANY] * count,
+        out_specs=ANY,
+        scratch_shapes=[
+            pltpu.VMEM((count * QUARTER, TOTAL), BF),
+            pltpu.VMEM((count * 3 * RES, COPM * GROUP * COPM), BF),
+            pltpu.VMEM((count * 4 * OWN, RES, CZ), F32),
+            pltpu.SemaphoreType.DMA((count,)),
+            pltpu.SemaphoreType.DMA((count * 4,)),
+        ],
+        compiler_params=pltpu.CompilerParams(vmem_limit_bytes=28 * MIB),
+        name="pair",
+    )(place, res_mask, mask, wide, right_all, *((own, other)[side][m] for m, side in quarters))
     added = pl.pallas_call(
         add_kernel,
         out_shape=jax.ShapeDtypeStruct((SEQ * RES, C), F32),
@@ -359,7 +363,7 @@
         compiler_params=pltpu.CompilerParams(vmem_limit_bytes=16 * MIB),
         name="add",
     )(tokens, output_weight, mixed)
-    return added.reshape(SEQ, RES, C), pair[0]
+    return added.reshape(SEQ, RES, C), pair
 
 
 FIRST = (1, 7, 3, 5, 4, 2, 6)

time: 113 us -> 112 us (level)
  starting transfers between devices: 48.2 us -> 56.1 us
  waiting for transfers between devices: 27.8 us -> 20.4 us
  Pallas kernels: 29.1 us -> 27.7 us
    ppermute x3, waiting for transfers between devices: 10.2 us -> 0.14 us  [shards(): own[m] = lax.ppermute(own[0], 'col', shift_x(m))]
    ppermute x4, starting transfers between devices: 8.92 us -> 18.7 us  [shards(): other = {m: lax.ppermute(own[m], 'col', SWAP) for m in range(4)}]
    ppermute x4, waiting for transfers between devices: 12.3 us -> 15 us  [shards(): along_z = [lax.ppermute(left, ('row', 'col'), scatter(n)) for n in range(4)]]
    ppermute x4, starting transfers between devices: 20.6 us -> 19 us  [shards(): along_z = [lax.ppermute(left, ('row', 'col'), scatter(n)) for n in range(4)]]
    pallas_call x2 -> x1, Pallas kernels: 11.4 us -> 9.93 us  [shards(): pl.pallas_call(functools.partial(pair_kernel, quarters), out_shape=jax.Sh...]
  transfers between devices with their start and end apart: 19 -> 19, of which waited for: 9 -> 8; matrix products, arithmetic and copies ran while one was open for 0% -> 0% of each run, Pallas kernels for 9% -> 3%
where the time goes in v2:
time: 112 us
  starting transfers between devices  56.1 us (50%)
  Pallas kernels  27.7 us (25%)
  waiting for transfers between devices  20.4 us (18%)
  local copies, waits for them, and re-layouts  6.54 us (6%)
    ppermute x4, starting transfers between devices, shards(): along_z = [lax.ppermute(left, ('row', 'col'), scatter(n)) for n in range(4)]  19 us
    ppermute x4, starting transfers between devices, shards(): other = {m: lax.ppermute(own[m], 'col', SWAP) for m in range(4)}  18.7 us
    ppermute x4, waiting for transfers between devices, shards(): along_z = [lax.ppermute(left, ('row', 'col'), scatter(n)) for n in range(4)]  15 us
    pallas_call x1, Pallas kernels, shards(): pl.pallas_call(attend_kernel, out_shape=[jax.ShapeDtypeStruct((ROWS, BLOC...  12.1 us
    pallas_call x1, Pallas kernels, shards(): pl.pallas_call(functools.partial(pair_kernel, quarters), out_shape=jax.Sh...  9.93 us
    ppermute x7, starting transfers between devices, shards(): blocks[ROWS - n] = lax.ppermute(sent[n], 'row', shift(n))  9.73 us
    unnamed x43, local copies, waits for them, and re-layouts  6.54 us
    all_to_all x1, starting transfers between devices, exchanged(): lax.all_to_all(values, 'row', split_axis=0, concat_axis=0, tiled=True)  5.96 us
  transfers between devices with their start and end apart: 19, of which 8 were waited for; matrix products, arithmetic and copies ran while one was open for 0% of the time, Pallas kernels for 3%

profile of v2, /device:TPU:41, one launch (start us, length us, event | category | flops | bytes accessed | tf_op | source)
XLA Modules:
  0.0 111.9 jit_solution(5772062356631073715)
XLA Ops:
  0.8 1.4 %copy-done.2 = f32[64,24,256]{2,1,0:T(8,128)S(1)} copy-done((f32[64,24,256]{2,1,0:T(8,128)S(1)}, f32[64,24,256]{2,1,0:T(8,128)}, u32[]{:S(2)}) %copy-start.2) | copy-done | bytes 1572888
  2.9 2.4 %norm.1 = (bf16[208,256]{1,0:T(8,128)(2,1)S(1)}, bf16[208,256]{1,0:T(8,128)(2,1)S(1)}, bf16[208,256]{1,0:T(8,128)(2,1)S(1)}, bf16[208,256]{1,0:T(8,128)(2,1)S(1)...) custom-call(s32[2]{0:T(128)S(1)} %pad_add_fusion.place_ref.refs_0_, ...), custom_call_target="tpu_custom_call" | custom-call | tf_op jit(solution)/shard_map/norm/pallas_call | solution.py:277
  5.5 1.9 %collective-permute-start.1 = (bf16[208,256]{1,0:T(8,128)(2,1)S(1)}, bf16[208,256]{1,0:T(8,128)(2,1)S(1)}, u32[]{:S(2)}, u32[]{:S(2)}) collective-permute-start(bf16[208,256]{1,0:T(8,128)(2,1)S(1)} %get-tuple-element.14), channel_id=1, source_target_pairs={{0,192},{32,224},{64,0},{96,32},{128,64},{160,96},{192,128},{224,1... | collective-permute-start | bytes 319496 | tf_op jit(solution)/shard_map/ppermute | solution.py:288
  7.4 3.0 %collective-permute-start.2 = (bf16[208,256]{1,0:T(8,128)(2,1)S(1)}, bf16[208,256]{1,0:T(8,128)(2,1)S(1)}, u32[]{:S(2)}, u32[]{:S(2)}) collective-permute-start(bf16[208,256]{1,0:T(8,128)(2,1)S(1)} %get-tuple-element.15), channel_id=1, source_target_pairs={{0,160},{32,192},{64,224},{96,0},{128,32},{160,64},{192,96},{224,1... | collective-permute-start | bytes 319496 | tf_op jit(solution)/shard_map/ppermute | solution.py:288
  11.4 2.0 %collective-permute-start.5 = (bf16[208,256]{1,0:T(8,128)(2,1)S(1)}, bf16[208,256]{1,0:T(8,128)(2,1)S(1)}, u32[]{:S(2)}, u32[]{:S(2)}) collective-permute-start(bf16[208,256]{1,0:T(8,128)(2,1)S(1)} %get-tuple-element.18), channel_id=1, source_target_pairs={{0,64},{32,96},{64,128},{96,160},{128,192},{160,224},{192,0},{224,... | collective-permute-start | bytes 319496 | tf_op jit(solution)/shard_map/ppermute | solution.py:288
  13.4 1.6 %collective-permute-start.6 = (bf16[208,256]{1,0:T(8,128)(2,1)S(1)}, bf16[208,256]{1,0:T(8,128)(2,1)S(1)}, u32[]{:S(2)}, u32[]{:S(2)}) collective-permute-start(bf16[208,256]{1,0:T(8,128)(2,1)S(1)} %get-tuple-element.19), channel_id=1, source_target_pairs={{0,32},{32,64},{64,96},{96,128},{128,160},{160,192},{192,224},{224... | collective-permute-start | bytes 319496 | tf_op jit(solution)/shard_map/ppermute | solution.py:288
  17.0 1.3 %collective-permute-done.5.refs_8_ = bf16[208,256]{1,0:T(8,128)(2,1)S(1)} collective-permute-done((bf16[208,256]{1,0:T(8,128)(2,1)S(1)}, bf16[208,256]{1,0:T(8,128)(2,1)S(1)}, u32[]{:S(2)}, u32[]{:S(2)}) %collective-permute-start.5) | collective-permute-done | bytes 106528 | tf_op jit(solution)/shard_map/ppermute | solution.py:288
  18.4 2.1 %collective-permute-done.6.refs_9_ = bf16[208,256]{1,0:T(8,128)(2,1)S(1)} collective-permute-done((bf16[208,256]{1,0:T(8,128)(2,1)S(1)}, bf16[208,256]{1,0:T(8,128)(2,1)S(1)}, u32[]{:S(2)}, u32[]{:S(2)}) %collective-permute-start.6) | collective-permute-done | bytes 106528 | tf_op jit(solution)/shard_map/ppermute | solution.py:288
  20.6 12.1 %attend.1 = (bf16[8,384,256]{2,1,0:T(8,128)(2,1)}, bf16[96,512]{1,0:T(8,128)(2,1)S(1)}) custom-call(s32[2]{0:T(128)S(1)} %pad_add_fusion.place_ref.refs_0_, s32[768]{0:T(1024)S(1)} %copy-done.12, bf16[208,256]{1,0:T(8,128)(2,1)S(1)} %get-tuple-element.12.refs_2_, bf16[208,256]{1,0:T(8,128)(2,1)S(1)} %collective-permute-done.refs_3_, ...), custom_call_target="tpu_custom_call" | custom-call | tf_op jit(solution)/shard_map/attend/pallas_call | solution.py:299
  32.7 6.0 %all-to-all-start = ((bf16[8,384,256]{2,1,0:T(8,128)(2,1)}), bf16[8,384,256]{2,1,0:T(8,128)(2,1)S(1)}, u32[]{:S(2)}, u32[]{:S(2)}) async-start(bf16[8,384,256]{2,1,0:T(8,128)(2,1)} %get-tuple-element.20), calls=%async_computation | async-start | bytes 3145728 | tf_op jit(solution)/shard_map/all_to_all | solution.py:373
  38.6 6.2 %collective-permute-start.7 = (bf16[96,512]{1,0:T(8,128)(2,1)S(1)}, bf16[96,512]{1,0:T(8,128)(2,1)S(1)}, u32[]{:S(2)}, u32[]{:S(2)}) collective-permute-start(bf16[96,512]{1,0:T(8,128)(2,1)S(1)} %get-tuple-element.21), channel_id=1, source_target_pairs={{0,0},{1,1},{2,2},{3,3},{4,36},{5,37},{6,38},{7,39},{8,64},{9,65},... | collective-permute-start | bytes 294920 | tf_op jit(solution)/shard_map/ppermute | solution.py:327
  44.9 1.9 %collective-permute-start.10 = (bf16[96,512]{1,0:T(8,128)(2,1)S(1)}, bf16[96,512]{1,0:T(8,128)(2,1)S(1)}, u32[]{:S(2)}, u32[]{:S(2)}) collective-permute-start(bf16[96,512]{1,0:T(8,128)(2,1)S(1)} %get-tuple-element.21), channel_id=1, source_target_pairs={{0,24},{1,25},{2,26},{3,27},{4,60},{5,61},{6,62},{7,63},{8,88},{9,... | collective-permute-start | bytes 294920 | tf_op jit(solution)/shard_map/ppermute | solution.py:327
  46.8 9.4 %collective-permute-start.9 = (bf16[96,512]{1,0:T(8,128)(2,1)S(1)}, bf16[96,512]{1,0:T(8,128)(2,1)S(1)}, u32[]{:S(2)}, u32[]{:S(2)}) collective-permute-start(bf16[96,512]{1,0:T(8,128)(2,1)S(1)} %get-tuple-element.21), channel_id=1, source_target_pairs={{0,16},{1,17},{2,18},{3,19},{4,52},{5,53},{6,54},{7,55},{8,80},{9,... | collective-permute-start | bytes 294920 | tf_op jit(solution)/shard_map/ppermute | solution.py:327
  56.2 1.4 %collective-permute-start.8 = (bf16[96,512]{1,0:T(8,128)(2,1)S(1)}, bf16[96,512]{1,0:T(8,128)(2,1)S(1)}, u32[]{:S(2)}, u32[]{:S(2)}) collective-permute-start(bf16[96,512]{1,0:T(8,128)(2,1)S(1)} %get-tuple-element.21), channel_id=1, source_target_pairs={{0,8},{1,9},{2,10},{3,11},{4,44},{5,45},{6,46},{7,47},{8,72},{9,73... | collective-permute-start | bytes 294920 | tf_op jit(solution)/shard_map/ppermute | solution.py:327
  57.6 10.2 %collective-permute-done.7 = bf16[96,512]{1,0:T(8,128)(2,1)S(1)} collective-permute-done((bf16[96,512]{1,0:T(8,128)(2,1)S(1)}, bf16[96,512]{1,0:T(8,128)(2,1)S(1)}, u32[]{:S(2)}, u32[]{:S(2)}) %collective-permute-start.7) | collective-permute-done | bytes 98336 | tf_op jit(solution)/shard_map/ppermute | solution.py:327
  67.9 3.9 %collective-permute-done.8 = bf16[96,512]{1,0:T(8,128)(2,1)S(1)} collective-permute-done((bf16[96,512]{1,0:T(8,128)(2,1)S(1)}, bf16[96,512]{1,0:T(8,128)(2,1)S(1)}, u32[]{:S(2)}, u32[]{:S(2)}) %collective-permute-start.8) | collective-permute-done | bytes 98336 | tf_op jit(solution)/shard_map/ppermute | solution.py:327
  72.8 2.7 %collective-permute-start.14 = (bf16[384,512]{1,0:T(8,128)(2,1)S(1)}, bf16[384,512]{1,0:T(8,128)(2,1)}, u32[]{:S(2)}, u32[]{:S(2)}) collective-permute-start(bf16[384,512]{1,0:T(8,128)(2,1)S(1)} %constant_dynamic-update-slice_fusion.refs_0_), channel_id=1, source_target_pairs={{0,6},{1,7},{2,0},{3,1},{4,2},{5,3},{6,4},{7,5},{8,14},{9,15},{10,... | collective-permute-start | bytes 1179656 | tf_op jit(solution)/shard_map/ppermute | solution.py:330
  75.5 5.5 %collective-permute-start.11 = (bf16[384,512]{1,0:T(8,128)(2,1)S(1)}, bf16[384,512]{1,0:T(8,128)(2,1)}, u32[]{:S(2)}, u32[]{:S(2)}) collective-permute-start(bf16[384,512]{1,0:T(8,128)(2,1)S(1)} %constant_dynamic-update-slice_fusion.refs_0_), channel_id=1, source_target_pairs={{0,1},{1,0},{2,3},{3,2},{4,5},{5,4},{6,7},{7,6},{8,9},{9,8},{10,11... | collective-permute-start | bytes 1179656 | tf_op jit(solution)/shard_map/ppermute | solution.py:331
  81.1 9.2 %collective-permute-start.17 = (bf16[384,512]{1,0:T(8,128)(2,1)}, bf16[384,512]{1,0:T(8,128)(2,1)}, u32[]{:S(2)}, u32[]{:S(2)}) collective-permute-start(bf16[384,512]{1,0:T(8,128)(2,1)} %collective-permute-done.16.refs_6_), channel_id=1, source_target_pairs={{0,1},{1,0},{2,3},{3,2},{4,5},{5,4},{6,7},{7,6},{8,9},{9,8},{10,11... | collective-permute-start | bytes 1179656 | tf_op jit(solution)/shard_map/ppermute | solution.py:331
  90.3 1.4 %collective-permute-start.15 = (bf16[384,512]{1,0:T(8,128)(2,1)}, bf16[384,512]{1,0:T(8,128)(2,1)}, u32[]{:S(2)}, u32[]{:S(2)}) collective-permute-start(bf16[384,512]{1,0:T(8,128)(2,1)} %collective-permute-done.14.refs_4_), channel_id=1, source_target_pairs={{0,1},{1,0},{2,3},{3,2},{4,5},{5,4},{6,7},{7,6},{8,9},{9,8},{10,11... | collective-permute-start | bytes 1179656 | tf_op jit(solution)/shard_map/ppermute | solution.py:331
  91.7 2.7 %collective-permute-start.13 = (bf16[384,512]{1,0:T(8,128)(2,1)}, bf16[384,512]{1,0:T(8,128)(2,1)}, u32[]{:S(2)}, u32[]{:S(2)}) collective-permute-start(bf16[384,512]{1,0:T(8,128)(2,1)} %collective-permute-done.12.refs_2_), channel_id=1, source_target_pairs={{0,1},{1,0},{2,3},{3,2},{4,5},{5,4},{6,7},{7,6},{8,9},{9,8},{10,11... | collective-permute-start | bytes 1179656 | tf_op jit(solution)/shard_map/ppermute | solution.py:331
  96.0 2.0 %copy-done = bf16[4096,512]{1,0:T(8,128)(2,1)} copy-done((bf16[4096,512]{1,0:T(8,128)(2,1)}, bf16[4096,512]{1,0:T(8,128)(2,1)S(1)}, u32[]{:S(2)}) %copy-start) | copy-done | bytes 4194328
  98.9 1.7 %add.3 = f32[1536,256]{1,0:T(8,128)} custom-call(f32[1536,256]{1,0:T(8,128)S(1)} %bitcast.8, bf16[256,256]{1,0:T(8,128)(2,1)S(1)} %copy-done.5, bf16[8,384,256]{2,1,0:T(8,128)(2,1)S(1)} %all-to-all-done.mixed_ref), custom_call_target="tpu_custom_call" | custom-call | tf_op jit(solution)/shard_map/add/pallas_call | solution.py:357
  101.8 9.9 %pair.1 = f32[96,24,128]{2,1,0:T(8,128)} custom-call(s32[2]{0:T(128)S(1)} %pad_add_fusion.place_ref.refs_0_, s32[768]{0:T(1024)S(1)} %copy-done.12, s32[1,512]{1,0:T(1,128)S(1)} %bitcast.10, bf16[4096,512]{1,0:T(8,128)(2,1)S(1)} %copy-done.1, bf16[768,512]{1,0:T(8,128)(2,1)S(1)} %order.1.right_ref, ...), custom_call_target="tpu_custom_call" | custom-call | tf_op jit(solution)/shard_map/pair/pallas_call | solution.py:342
  (65 shorter events, 8.9 us)
Async XLA Ops:
  0.6 19.9 %copy-start.15 = (f32[256]{0:T(256)S(1)}, f32[256]{0:T(256)}, u32[]{:S(2)}) copy-start(f32[256]{0:T(256)} %param.17) | copy-start | bytes 3076
  0.6 19.9 %copy-start.12 = (s32[768]{0:T(1024)S(1)}, s32[768]{0:T(1024)}, u32[]{:S(2)}) copy-start(s32[768]{0:T(1024)} %res_mask_ref.1) | copy-start | bytes 9220
  0.7 19.9 %copy-start.16 = (f32[256]{0:T(256)S(1)}, f32[256]{0:T(256)}, u32[]{:S(2)}) copy-start(f32[256]{0:T(256)} %param.18) | copy-start | bytes 3076
  0.7 19.8 %copy-start.13 = (s32[512]{0:T(512)S(1)}, s32[512]{0:T(512)}, u32[]{:S(2)}) copy-start(s32[512]{0:T(512)} %param.15) | copy-start | bytes 6148
  5.3 6.1 %collective-permute-start = (bf16[208,256]{1,0:T(8,128)(2,1)S(1)}, bf16[208,256]{1,0:T(8,128)(2,1)S(1)}, u32[]{:S(2)}, u32[]{:S(2)}) collective-permute-start(bf16[208,256]{1,0:T(8,128)(2,1)S(1)} %get-tuple-element.13), channel_id=1, source_target_pairs={{0,224},{32,0},{64,32},{96,64},{128,96},{160,128},{192,160},{224,1... | collective-permute-start | bytes 319496 | tf_op jit(solution)/shard_map/ppermute | solution.py:288
  5.5 7.9 %collective-permute-start.1 = (bf16[208,256]{1,0:T(8,128)(2,1)S(1)}, bf16[208,256]{1,0:T(8,128)(2,1)S(1)}, u32[]{:S(2)}, u32[]{:S(2)}) collective-permute-start(bf16[208,256]{1,0:T(8,128)(2,1)S(1)} %get-tuple-element.14), channel_id=1, source_target_pairs={{0,192},{32,224},{64,0},{96,32},{128,64},{160,96},{192,128},{224,1... | collective-permute-start | bytes 319496 | tf_op jit(solution)/shard_map/ppermute | solution.py:288
  7.4 8.7 %collective-permute-start.2 = (bf16[208,256]{1,0:T(8,128)(2,1)S(1)}, bf16[208,256]{1,0:T(8,128)(2,1)S(1)}, u32[]{:S(2)}, u32[]{:S(2)}) collective-permute-start(bf16[208,256]{1,0:T(8,128)(2,1)S(1)} %get-tuple-element.15), channel_id=1, source_target_pairs={{0,160},{32,192},{64,224},{96,0},{128,32},{160,64},{192,96},{224,1... | collective-permute-start | bytes 319496 | tf_op jit(solution)/shard_map/ppermute | solution.py:288
  10.3 5.8 %collective-permute-start.3 = (bf16[208,256]{1,0:T(8,128)(2,1)S(1)}, bf16[208,256]{1,0:T(8,128)(2,1)S(1)}, u32[]{:S(2)}, u32[]{:S(2)}) collective-permute-start(bf16[208,256]{1,0:T(8,128)(2,1)S(1)} %get-tuple-element.16), channel_id=1, source_target_pairs={{0,128},{32,160},{64,192},{96,224},{128,0},{160,32},{192,64},{224,... | collective-permute-start | bytes 319496 | tf_op jit(solution)/shard_map/ppermute | solution.py:288
  10.3 6.7 %collective-permute-start.4 = (bf16[208,256]{1,0:T(8,128)(2,1)S(1)}, bf16[208,256]{1,0:T(8,128)(2,1)S(1)}, u32[]{:S(2)}, u32[]{:S(2)}) collective-permute-start(bf16[208,256]{1,0:T(8,128)(2,1)S(1)} %get-tuple-element.17), channel_id=1, source_target_pairs={{0,96},{32,128},{64,160},{96,192},{128,224},{160,0},{192,32},{224,... | collective-permute-start | bytes 319496 | tf_op jit(solution)/shard_map/ppermute | solution.py:288
  11.4 7.0 %collective-permute-start.5 = (bf16[208,256]{1,0:T(8,128)(2,1)S(1)}, bf16[208,256]{1,0:T(8,128)(2,1)S(1)}, u32[]{:S(2)}, u32[]{:S(2)}) collective-permute-start(bf16[208,256]{1,0:T(8,128)(2,1)S(1)} %get-tuple-element.18), channel_id=1, source_target_pairs={{0,64},{32,96},{64,128},{96,160},{128,192},{160,224},{192,0},{224,... | collective-permute-start | bytes 319496 | tf_op jit(solution)/shard_map/ppermute | solution.py:288
  13.4 7.1 %collective-permute-start.6 = (bf16[208,256]{1,0:T(8,128)(2,1)S(1)}, bf16[208,256]{1,0:T(8,128)(2,1)S(1)}, u32[]{:S(2)}, u32[]{:S(2)}) collective-permute-start(bf16[208,256]{1,0:T(8,128)(2,1)S(1)} %get-tuple-element.19), channel_id=1, source_target_pairs={{0,32},{32,64},{64,96},{96,128},{128,160},{160,192},{192,224},{224... | collective-permute-start | bytes 319496 | tf_op jit(solution)/shard_map/ppermute | solution.py:288
  32.7 65.3 %all-to-all-start = ((bf16[8,384,256]{2,1,0:T(8,128)(2,1)}), bf16[8,384,256]{2,1,0:T(8,128)(2,1)S(1)}, u32[]{:S(2)}, u32[]{:S(2)}) async-start(bf16[8,384,256]{2,1,0:T(8,128)(2,1)} %get-tuple-element.20), calls=%async_computation | async-start | bytes 3145728 | tf_op jit(solution)/shard_map/all_to_all | solution.py:373
  38.6 29.2 %collective-permute-start.7 = (bf16[96,512]{1,0:T(8,128)(2,1)S(1)}, bf16[96,512]{1,0:T(8,128)(2,1)S(1)}, u32[]{:S(2)}, u32[]{:S(2)}) collective-permute-start(bf16[96,512]{1,0:T(8,128)(2,1)S(1)} %get-tuple-element.21), channel_id=1, source_target_pairs={{0,0},{1,1},{2,2},{3,3},{4,36},{5,37},{6,38},{7,39},{8,64},{9,65},... | collective-permute-start | bytes 294920 | tf_op jit(solution)/shard_map/ppermute | solution.py:327
  44.9 27.7 %collective-permute-start.10 = (bf16[96,512]{1,0:T(8,128)(2,1)S(1)}, bf16[96,512]{1,0:T(8,128)(2,1)S(1)}, u32[]{:S(2)}, u32[]{:S(2)}) collective-permute-start(bf16[96,512]{1,0:T(8,128)(2,1)S(1)} %get-tuple-element.21), channel_id=1, source_target_pairs={{0,24},{1,25},{2,26},{3,27},{4,60},{5,61},{6,62},{7,63},{8,88},{9,... | collective-permute-start | bytes 294920 | tf_op jit(solution)/shard_map/ppermute | solution.py:327
  46.8 25.8 %collective-permute-start.9 = (bf16[96,512]{1,0:T(8,128)(2,1)S(1)}, bf16[96,512]{1,0:T(8,128)(2,1)S(1)}, u32[]{:S(2)}, u32[]{:S(2)}) collective-permute-start(bf16[96,512]{1,0:T(8,128)(2,1)S(1)} %get-tuple-element.21), channel_id=1, source_target_pairs={{0,16},{1,17},{2,18},{3,19},{4,52},{5,53},{6,54},{7,55},{8,80},{9,... | collective-permute-start | bytes 294920 | tf_op jit(solution)/shard_map/ppermute | solution.py:327
  56.2 15.6 %collective-permute-start.8 = (bf16[96,512]{1,0:T(8,128)(2,1)S(1)}, bf16[96,512]{1,0:T(8,128)(2,1)S(1)}, u32[]{:S(2)}, u32[]{:S(2)}) collective-permute-start(bf16[96,512]{1,0:T(8,128)(2,1)S(1)} %get-tuple-element.21), channel_id=1, source_target_pairs={{0,8},{1,9},{2,10},{3,11},{4,44},{5,45},{6,46},{7,47},{8,72},{9,73... | collective-permute-start | bytes 294920 | tf_op jit(solution)/shard_map/ppermute | solution.py:327
  72.7 25.3 %copy-start.3 = (f32[64,24,256]{2,1,0:T(8,128)S(1)}, f32[64,24,256]{2,1,0:T(8,128)}, u32[]{:S(2)}) copy-start(f32[64,24,256]{2,1,0:T(8,128)} %param.14) | copy-start | bytes 4718596
  72.7 8.4 %collective-permute-start.16 = (bf16[384,512]{1,0:T(8,128)(2,1)S(1)}, bf16[384,512]{1,0:T(8,128)(2,1)}, u32[]{:S(2)}, u32[]{:S(2)}) collective-permute-start(bf16[384,512]{1,0:T(8,128)(2,1)S(1)} %constant_dynamic-update-slice_fusion.refs_0_), channel_id=1, source_target_pairs={{0,4},{1,5},{2,6},{3,7},{4,0},{5,1},{6,2},{7,3},{8,12},{9,13},{10,... | collective-permute-start | bytes 1179656 | tf_op jit(solution)/shard_map/ppermute | solution.py:330
  72.8 17.5 %collective-permute-start.14 = (bf16[384,512]{1,0:T(8,128)(2,1)S(1)}, bf16[384,512]{1,0:T(8,128)(2,1)}, u32[]{:S(2)}, u32[]{:S(2)}) collective-permute-start(bf16[384,512]{1,0:T(8,128)(2,1)S(1)} %constant_dynamic-update-slice_fusion.refs_0_), channel_id=1, source_target_pairs={{0,6},{1,7},{2,0},{3,1},{4,2},{5,3},{6,4},{7,5},{8,14},{9,15},{10,... | collective-permute-start | bytes 1179656 | tf_op jit(solution)/shard_map/ppermute | solution.py:330
  75.5 16.2 %collective-permute-start.12 = (bf16[384,512]{1,0:T(8,128)(2,1)S(1)}, bf16[384,512]{1,0:T(8,128)(2,1)}, u32[]{:S(2)}, u32[]{:S(2)}) collective-permute-start(bf16[384,512]{1,0:T(8,128)(2,1)S(1)} %constant_dynamic-update-slice_fusion.refs_0_), channel_id=1, source_target_pairs={{0,2},{1,3},{2,4},{3,5},{4,6},{5,7},{6,0},{7,1},{8,10},{9,11},{10,... | collective-permute-start | bytes 1179656 | tf_op jit(solution)/shard_map/ppermute | solution.py:330
  75.5 26.0 %collective-permute-start.11 = (bf16[384,512]{1,0:T(8,128)(2,1)S(1)}, bf16[384,512]{1,0:T(8,128)(2,1)}, u32[]{:S(2)}, u32[]{:S(2)}) collective-permute-start(bf16[384,512]{1,0:T(8,128)(2,1)S(1)} %constant_dynamic-update-slice_fusion.refs_0_), channel_id=1, source_target_pairs={{0,1},{1,0},{2,3},{3,2},{4,5},{5,4},{6,7},{7,6},{8,9},{9,8},{10,11... | collective-permute-start | bytes 1179656 | tf_op jit(solution)/shard_map/ppermute | solution.py:331
  81.1 20.3 %collective-permute-start.17 = (bf16[384,512]{1,0:T(8,128)(2,1)}, bf16[384,512]{1,0:T(8,128)(2,1)}, u32[]{:S(2)}, u32[]{:S(2)}) collective-permute-start(bf16[384,512]{1,0:T(8,128)(2,1)} %collective-permute-done.16.refs_6_), channel_id=1, source_target_pairs={{0,1},{1,0},{2,3},{3,2},{4,5},{5,4},{6,7},{7,6},{8,9},{9,8},{10,11... | collective-permute-start | bytes 1179656 | tf_op jit(solution)/shard_map/ppermute | solution.py:331
  90.3 11.2 %collective-permute-start.15 = (bf16[384,512]{1,0:T(8,128)(2,1)}, bf16[384,512]{1,0:T(8,128)(2,1)}, u32[]{:S(2)}, u32[]{:S(2)}) collective-permute-start(bf16[384,512]{1,0:T(8,128)(2,1)} %collective-permute-done.14.refs_4_), channel_id=1, source_target_pairs={{0,1},{1,0},{2,3},{3,2},{4,5},{5,4},{6,7},{7,6},{8,9},{9,8},{10,11... | collective-permute-start | bytes 1179656 | tf_op jit(solution)/shard_map/ppermute | solution.py:331
  91.7 9.8 %collective-permute-start.13 = (bf16[384,512]{1,0:T(8,128)(2,1)}, bf16[384,512]{1,0:T(8,128)(2,1)}, u32[]{:S(2)}, u32[]{:S(2)}) collective-permute-start(bf16[384,512]{1,0:T(8,128)(2,1)} %collective-permute-done.12.refs_2_), channel_id=1, source_target_pairs={{0,1},{1,0},{2,3},{3,2},{4,5},{5,4},{6,7},{7,6},{8,9},{9,8},{10,11... | collective-permute-start | bytes 1179656 | tf_op jit(solution)/shard_map/ppermute | solution.py:331
  (14 other events, 123.4 us)

commit v3 on v2

--- a/solution.py
+++ b/solution.py
@@ -2,7 +2,6 @@
 
 import jax
 import jax.numpy as jnp
-import numpy as np
 from jax import lax
 from jax.experimental import pallas as pl
 from jax.experimental.pallas import tpu as pltpu
@@ -157,8 +156,13 @@
             out_ref[start : start + COPM, i * CZ : (i + 1) * CZ] = part
 
 
-def order_kernel(order_ref, mixed_ref, out_ref):
-    pick = (order_ref[...] == iota((RES * COPM, RES * COPM), 1)).astype(BF)
+def order_kernel(mixed_ref, out_ref):
+    place = iota((RES * COPM, 128), 0)[:, 0:1].astype(F32)
+    channel = jnp.floor((place + 0.5) * (1.0 / RES))
+    residue = place - channel * RES
+    device = jnp.floor((residue + 0.5) * (1.0 / OWN))
+    source = (device * SIDE + (residue - device * OWN) * COPM + channel).astype(jnp.int32)
+    pick = (source == iota((RES * COPM, RES * COPM), 1)).astype(BF)
     for i in range(2):
         start = BLOCK + i * SIDE
         part = jnp.concatenate([mixed_ref[n, start : start + SIDE, :] for n in range(ROWS)], 0)
@@ -251,11 +255,6 @@
     return pairs
 
 
-ORDER = np.array(
-    [[j // OWN * SIDE + j % OWN * COPM + b] for b in range(COPM) for j in range(RES)], np.int32
-)
-
-
 def shards(
     alignment,
     seq_mask,
@@ -332,11 +331,11 @@
     right_all = pl.pallas_call(
         order_kernel,
         out_shape=jax.ShapeDtypeStruct((RES * COPM, TOTAL), BF),
-        in_specs=[VMEM] * 2,
+        in_specs=[VMEM],
         out_specs=VMEM,
         compiler_params=pltpu.CompilerParams(vmem_limit_bytes=16 * MIB),
         name="order",
-    )(ORDER, mixed)
+    )(mixed)
     quarters = [(m, side) for m in (0, 1, 3, 2) for side in range(2)]
     count = len(quarters)
     pair = pl.pallas_call(

time: 112 us -> 112 us (level)
    unnamed x43 -> x41, local copies, waits for them, and re-layouts: 6.54 us -> 5.95 us
where the time goes in v3:
time: 112 us; the launch traced here: 111 us
  starting transfers between devices  56.3 us (50%)
  Pallas kernels  27.7 us (25%)
  waiting for transfers between devices  20.4 us (18%)
  local copies, waits for them, and re-layouts  5.95 us (5%)
    ppermute x4, starting transfers between devices, shards(): along_z = [lax.ppermute(left, ('row', 'col'), scatter(n)) for n in range(4)]  19 us
    ppermute x4, starting transfers between devices, shards(): other = {m: lax.ppermute(own[m], 'col', SWAP) for m in range(4)}  18.7 us
    ppermute x4, waiting for transfers between devices, shards(): along_z = [lax.ppermute(left, ('row', 'col'), scatter(n)) for n in range(4)]  15 us
    pallas_call x1, Pallas kernels, shards(): pl.pallas_call(attend_kernel, out_shape=[jax.ShapeDtypeStruct((ROWS, BLOC...  12.1 us
    pallas_call x1, Pallas kernels, shards(): pl.pallas_call(functools.partial(pair_kernel, quarters), out_shape=jax.Sh...  9.93 us
    ppermute x7, starting transfers between devices, shards(): blocks[ROWS - n] = lax.ppermute(sent[n], 'row', shift(n))  9.73 us
    all_to_all x1, starting transfers between devices, exchanged(): lax.all_to_all(values, 'row', split_axis=0, concat_axis=0, tiled=True)  6.09 us
    unnamed x41, local copies, waits for them, and re-layouts  5.95 us
  transfers between devices with their start and end apart: 19, of which 8 were waited for; matrix products, arithmetic and copies ran while one was open for 0% of the time, Pallas kernels for 3%

profile of v3, /device:TPU:41, one launch (start us, length us, event | category | flops | bytes accessed | tf_op | source)
XLA Modules:
  0.0 111.4 jit_solution(6544510279163336429)
XLA Ops:
  0.8 1.4 %copy-done.2 = f32[64,24,256]{2,1,0:T(8,128)S(1)} copy-done((f32[64,24,256]{2,1,0:T(8,128)S(1)}, f32[64,24,256]{2,1,0:T(8,128)}, u32[]{:S(2)}) %copy-start.2) | copy-done | bytes 1572888
  2.9 2.4 %norm.1 = (bf16[208,256]{1,0:T(8,128)(2,1)S(1)}, bf16[208,256]{1,0:T(8,128)(2,1)S(1)}, bf16[208,256]{1,0:T(8,128)(2,1)S(1)}, bf16[208,256]{1,0:T(8,128)(2,1)S(1)...) custom-call(s32[2]{0:T(128)S(1)} %pad_add_fusion.place_ref.refs_0_, ...), custom_call_target="tpu_custom_call" | custom-call | tf_op jit(solution)/shard_map/norm/pallas_call | solution.py:276
  5.5 1.9 %collective-permute-start.1 = (bf16[208,256]{1,0:T(8,128)(2,1)S(1)}, bf16[208,256]{1,0:T(8,128)(2,1)S(1)}, u32[]{:S(2)}, u32[]{:S(2)}) collective-permute-start(bf16[208,256]{1,0:T(8,128)(2,1)S(1)} %get-tuple-element.14), channel_id=1, source_target_pairs={{0,192},{32,224},{64,0},{96,32},{128,64},{160,96},{192,128},{224,1... | collective-permute-start | bytes 319496 | tf_op jit(solution)/shard_map/ppermute | solution.py:287
  7.4 3.0 %collective-permute-start.2 = (bf16[208,256]{1,0:T(8,128)(2,1)S(1)}, bf16[208,256]{1,0:T(8,128)(2,1)S(1)}, u32[]{:S(2)}, u32[]{:S(2)}) collective-permute-start(bf16[208,256]{1,0:T(8,128)(2,1)S(1)} %get-tuple-element.15), channel_id=1, source_target_pairs={{0,160},{32,192},{64,224},{96,0},{128,32},{160,64},{192,96},{224,1... | collective-permute-start | bytes 319496 | tf_op jit(solution)/shard_map/ppermute | solution.py:287
  11.4 2.0 %collective-permute-start.5 = (bf16[208,256]{1,0:T(8,128)(2,1)S(1)}, bf16[208,256]{1,0:T(8,128)(2,1)S(1)}, u32[]{:S(2)}, u32[]{:S(2)}) collective-permute-start(bf16[208,256]{1,0:T(8,128)(2,1)S(1)} %get-tuple-element.18), channel_id=1, source_target_pairs={{0,64},{32,96},{64,128},{96,160},{128,192},{160,224},{192,0},{224,... | collective-permute-start | bytes 319496 | tf_op jit(solution)/shard_map/ppermute | solution.py:287
  13.4 1.6 %collective-permute-start.6 = (bf16[208,256]{1,0:T(8,128)(2,1)S(1)}, bf16[208,256]{1,0:T(8,128)(2,1)S(1)}, u32[]{:S(2)}, u32[]{:S(2)}) collective-permute-start(bf16[208,256]{1,0:T(8,128)(2,1)S(1)} %get-tuple-element.19), channel_id=1, source_target_pairs={{0,32},{32,64},{64,96},{96,128},{128,160},{160,192},{192,224},{224... | collective-permute-start | bytes 319496 | tf_op jit(solution)/shard_map/ppermute | solution.py:287
  17.0 1.3 %collective-permute-done.5.refs_8_ = bf16[208,256]{1,0:T(8,128)(2,1)S(1)} collective-permute-done((bf16[208,256]{1,0:T(8,128)(2,1)S(1)}, bf16[208,256]{1,0:T(8,128)(2,1)S(1)}, u32[]{:S(2)}, u32[]{:S(2)}) %collective-permute-start.5) | collective-permute-done | bytes 106528 | tf_op jit(solution)/shard_map/ppermute | solution.py:287
  18.4 2.1 %collective-permute-done.6.refs_9_ = bf16[208,256]{1,0:T(8,128)(2,1)S(1)} collective-permute-done((bf16[208,256]{1,0:T(8,128)(2,1)S(1)}, bf16[208,256]{1,0:T(8,128)(2,1)S(1)}, u32[]{:S(2)}, u32[]{:S(2)}) %collective-permute-start.6) | collective-permute-done | bytes 106528 | tf_op jit(solution)/shard_map/ppermute | solution.py:287
  20.6 12.1 %attend.1 = (bf16[8,384,256]{2,1,0:T(8,128)(2,1)}, bf16[96,512]{1,0:T(8,128)(2,1)S(1)}) custom-call(s32[2]{0:T(128)S(1)} %pad_add_fusion.place_ref.refs_0_, s32[768]{0:T(1024)S(1)} %copy-done.11, bf16[208,256]{1,0:T(8,128)(2,1)S(1)} %get-tuple-element.12.refs_2_, bf16[208,256]{1,0:T(8,128)(2,1)S(1)} %collective-permute-done.refs_3_, ...), custom_call_target="tpu_custom_call" | custom-call | tf_op jit(solution)/shard_map/attend/pallas_call | solution.py:298
  32.7 6.1 %all-to-all-start = ((bf16[8,384,256]{2,1,0:T(8,128)(2,1)}), bf16[8,384,256]{2,1,0:T(8,128)(2,1)S(1)}, u32[]{:S(2)}, u32[]{:S(2)}) async-start(bf16[8,384,256]{2,1,0:T(8,128)(2,1)} %get-tuple-element.20), calls=%async_computation | async-start | bytes 3145728 | tf_op jit(solution)/shard_map/all_to_all | solution.py:372
  38.8 6.2 %collective-permute-start.7 = (bf16[96,512]{1,0:T(8,128)(2,1)S(1)}, bf16[96,512]{1,0:T(8,128)(2,1)S(1)}, u32[]{:S(2)}, u32[]{:S(2)}) collective-permute-start(bf16[96,512]{1,0:T(8,128)(2,1)S(1)} %get-tuple-element.21), channel_id=1, source_target_pairs={{0,0},{1,1},{2,2},{3,3},{4,36},{5,37},{6,38},{7,39},{8,64},{9,65},... | collective-permute-start | bytes 294920 | tf_op jit(solution)/shard_map/ppermute | solution.py:326
  45.0 1.9 %collective-permute-start.10 = (bf16[96,512]{1,0:T(8,128)(2,1)S(1)}, bf16[96,512]{1,0:T(8,128)(2,1)S(1)}, u32[]{:S(2)}, u32[]{:S(2)}) collective-permute-start(bf16[96,512]{1,0:T(8,128)(2,1)S(1)} %get-tuple-element.21), channel_id=1, source_target_pairs={{0,24},{1,25},{2,26},{3,27},{4,60},{5,61},{6,62},{7,63},{8,88},{9,... | collective-permute-start | bytes 294920 | tf_op jit(solution)/shard_map/ppermute | solution.py:326
  47.0 9.4 %collective-permute-start.9 = (bf16[96,512]{1,0:T(8,128)(2,1)S(1)}, bf16[96,512]{1,0:T(8,128)(2,1)S(1)}, u32[]{:S(2)}, u32[]{:S(2)}) collective-permute-start(bf16[96,512]{1,0:T(8,128)(2,1)S(1)} %get-tuple-element.21), channel_id=1, source_target_pairs={{0,16},{1,17},{2,18},{3,19},{4,52},{5,53},{6,54},{7,55},{8,80},{9,... | collective-permute-start | bytes 294920 | tf_op jit(solution)/shard_map/ppermute | solution.py:326
  56.3 1.4 %collective-permute-start.8 = (bf16[96,512]{1,0:T(8,128)(2,1)S(1)}, bf16[96,512]{1,0:T(8,128)(2,1)S(1)}, u32[]{:S(2)}, u32[]{:S(2)}) collective-permute-start(bf16[96,512]{1,0:T(8,128)(2,1)S(1)} %get-tuple-element.21), channel_id=1, source_target_pairs={{0,8},{1,9},{2,10},{3,11},{4,44},{5,45},{6,46},{7,47},{8,72},{9,73... | collective-permute-start | bytes 294920 | tf_op jit(solution)/shard_map/ppermute | solution.py:326
  57.8 10.2 %collective-permute-done.7 = bf16[96,512]{1,0:T(8,128)(2,1)S(1)} collective-permute-done((bf16[96,512]{1,0:T(8,128)(2,1)S(1)}, bf16[96,512]{1,0:T(8,128)(2,1)S(1)}, u32[]{:S(2)}, u32[]{:S(2)}) %collective-permute-start.7) | collective-permute-done | bytes 98336 | tf_op jit(solution)/shard_map/ppermute | solution.py:326
  68.0 3.9 %collective-permute-done.8 = bf16[96,512]{1,0:T(8,128)(2,1)S(1)} collective-permute-done((bf16[96,512]{1,0:T(8,128)(2,1)S(1)}, bf16[96,512]{1,0:T(8,128)(2,1)S(1)}, u32[]{:S(2)}, u32[]{:S(2)}) %collective-permute-start.8) | collective-permute-done | bytes 98336 | tf_op jit(solution)/shard_map/ppermute | solution.py:326
  72.9 2.7 %collective-permute-start.14 = (bf16[384,512]{1,0:T(8,128)(2,1)S(1)}, bf16[384,512]{1,0:T(8,128)(2,1)}, u32[]{:S(2)}, u32[]{:S(2)}) collective-permute-start(bf16[384,512]{1,0:T(8,128)(2,1)S(1)} %constant_dynamic-update-slice_fusion.refs_0_), channel_id=1, source_target_pairs={{0,6},{1,7},{2,0},{3,1},{4,2},{5,3},{6,4},{7,5},{8,14},{9,15},{10,... | collective-permute-start | bytes 1179656 | tf_op jit(solution)/shard_map/ppermute | solution.py:329
  75.6 5.5 %collective-permute-start.11 = (bf16[384,512]{1,0:T(8,128)(2,1)S(1)}, bf16[384,512]{1,0:T(8,128)(2,1)}, u32[]{:S(2)}, u32[]{:S(2)}) collective-permute-start(bf16[384,512]{1,0:T(8,128)(2,1)S(1)} %constant_dynamic-update-slice_fusion.refs_0_), channel_id=1, source_target_pairs={{0,1},{1,0},{2,3},{3,2},{4,5},{5,4},{6,7},{7,6},{8,9},{9,8},{10,11... | collective-permute-start | bytes 1179656 | tf_op jit(solution)/shard_map/ppermute | solution.py:330
  81.2 9.2 %collective-permute-start.17 = (bf16[384,512]{1,0:T(8,128)(2,1)}, bf16[384,512]{1,0:T(8,128)(2,1)}, u32[]{:S(2)}, u32[]{:S(2)}) collective-permute-start(bf16[384,512]{1,0:T(8,128)(2,1)} %collective-permute-done.16.refs_6_), channel_id=1, source_target_pairs={{0,1},{1,0},{2,3},{3,2},{4,5},{5,4},{6,7},{7,6},{8,9},{9,8},{10,11... | collective-permute-start | bytes 1179656 | tf_op jit(solution)/shard_map/ppermute | solution.py:330
  90.4 1.4 %collective-permute-start.15 = (bf16[384,512]{1,0:T(8,128)(2,1)}, bf16[384,512]{1,0:T(8,128)(2,1)}, u32[]{:S(2)}, u32[]{:S(2)}) collective-permute-start(bf16[384,512]{1,0:T(8,128)(2,1)} %collective-permute-done.14.refs_4_), channel_id=1, source_target_pairs={{0,1},{1,0},{2,3},{3,2},{4,5},{5,4},{6,7},{7,6},{8,9},{9,8},{10,11... | collective-permute-start | bytes 1179656 | tf_op jit(solution)/shard_map/ppermute | solution.py:330
  91.8 2.7 %collective-permute-start.13 = (bf16[384,512]{1,0:T(8,128)(2,1)}, bf16[384,512]{1,0:T(8,128)(2,1)}, u32[]{:S(2)}, u32[]{:S(2)}) collective-permute-start(bf16[384,512]{1,0:T(8,128)(2,1)} %collective-permute-done.12.refs_2_), channel_id=1, source_target_pairs={{0,1},{1,0},{2,3},{3,2},{4,5},{5,4},{6,7},{7,6},{8,9},{9,8},{10,11... | collective-permute-start | bytes 1179656 | tf_op jit(solution)/shard_map/ppermute | solution.py:330
  95.2 2.0 %copy-done = bf16[4096,512]{1,0:T(8,128)(2,1)} copy-done((bf16[4096,512]{1,0:T(8,128)(2,1)}, bf16[4096,512]{1,0:T(8,128)(2,1)S(1)}, u32[]{:S(2)}) %copy-start) | copy-done | bytes 4194328
  98.6 1.7 %add.3 = f32[1536,256]{1,0:T(8,128)} custom-call(f32[1536,256]{1,0:T(8,128)S(1)} %bitcast.8, bf16[256,256]{1,0:T(8,128)(2,1)S(1)} %copy-done.5, bf16[8,384,256]{2,1,0:T(8,128)(2,1)S(1)} %all-to-all-done.mixed_ref), custom_call_target="tpu_custom_call" | custom-call | tf_op jit(solution)/shard_map/add/pallas_call | solution.py:356
  101.3 9.9 %pair.1 = f32[96,24,128]{2,1,0:T(8,128)} custom-call(s32[2]{0:T(128)S(1)} %pad_add_fusion.place_ref.refs_0_, s32[768]{0:T(1024)S(1)} %copy-done.11, s32[1,512]{1,0:T(1,128)S(1)} %bitcast.10, bf16[4096,512]{1,0:T(8,128)(2,1)S(1)} %copy-done.1, bf16[768,512]{1,0:T(8,128)(2,1)S(1)} %order.1.right_ref, ...), custom_call_target="tpu_custom_call" | custom-call | tf_op jit(solution)/shard_map/pair/pallas_call | solution.py:341
  (63 shorter events, 8.3 us)
Async XLA Ops:
  0.6 19.9 %copy-start.14 = (f32[256]{0:T(256)S(1)}, f32[256]{0:T(256)}, u32[]{:S(2)}) copy-start(f32[256]{0:T(256)} %param.16) | copy-start | bytes 3076
  0.6 19.9 %copy-start.11 = (s32[768]{0:T(1024)S(1)}, s32[768]{0:T(1024)}, u32[]{:S(2)}) copy-start(s32[768]{0:T(1024)} %res_mask_ref.1) | copy-start | bytes 9220
  0.7 19.9 %copy-start.15 = (f32[256]{0:T(256)S(1)}, f32[256]{0:T(256)}, u32[]{:S(2)}) copy-start(f32[256]{0:T(256)} %param.17) | copy-start | bytes 3076
  0.7 19.8 %copy-start.12 = (s32[512]{0:T(512)S(1)}, s32[512]{0:T(512)}, u32[]{:S(2)}) copy-start(s32[512]{0:T(512)} %param.14) | copy-start | bytes 6148
  5.3 6.1 %collective-permute-start = (bf16[208,256]{1,0:T(8,128)(2,1)S(1)}, bf16[208,256]{1,0:T(8,128)(2,1)S(1)}, u32[]{:S(2)}, u32[]{:S(2)}) collective-permute-start(bf16[208,256]{1,0:T(8,128)(2,1)S(1)} %get-tuple-element.13), channel_id=1, source_target_pairs={{0,224},{32,0},{64,32},{96,64},{128,96},{160,128},{192,160},{224,1... | collective-permute-start | bytes 319496 | tf_op jit(solution)/shard_map/ppermute | solution.py:287
  5.5 7.9 %collective-permute-start.1 = (bf16[208,256]{1,0:T(8,128)(2,1)S(1)}, bf16[208,256]{1,0:T(8,128)(2,1)S(1)}, u32[]{:S(2)}, u32[]{:S(2)}) collective-permute-start(bf16[208,256]{1,0:T(8,128)(2,1)S(1)} %get-tuple-element.14), channel_id=1, source_target_pairs={{0,192},{32,224},{64,0},{96,32},{128,64},{160,96},{192,128},{224,1... | collective-permute-start | bytes 319496 | tf_op jit(solution)/shard_map/ppermute | solution.py:287
  7.4 8.7 %collective-permute-start.2 = (bf16[208,256]{1,0:T(8,128)(2,1)S(1)}, bf16[208,256]{1,0:T(8,128)(2,1)S(1)}, u32[]{:S(2)}, u32[]{:S(2)}) collective-permute-start(bf16[208,256]{1,0:T(8,128)(2,1)S(1)} %get-tuple-element.15), channel_id=1, source_target_pairs={{0,160},{32,192},{64,224},{96,0},{128,32},{160,64},{192,96},{224,1... | collective-permute-start | bytes 319496 | tf_op jit(solution)/shard_map/ppermute | solution.py:287
  10.3 5.8 %collective-permute-start.3 = (bf16[208,256]{1,0:T(8,128)(2,1)S(1)}, bf16[208,256]{1,0:T(8,128)(2,1)S(1)}, u32[]{:S(2)}, u32[]{:S(2)}) collective-permute-start(bf16[208,256]{1,0:T(8,128)(2,1)S(1)} %get-tuple-element.16), channel_id=1, source_target_pairs={{0,128},{32,160},{64,192},{96,224},{128,0},{160,32},{192,64},{224,... | collective-permute-start | bytes 319496 | tf_op jit(solution)/shard_map/ppermute | solution.py:287
  10.3 6.7 %collective-permute-start.4 = (bf16[208,256]{1,0:T(8,128)(2,1)S(1)}, bf16[208,256]{1,0:T(8,128)(2,1)S(1)}, u32[]{:S(2)}, u32[]{:S(2)}) collective-permute-start(bf16[208,256]{1,0:T(8,128)(2,1)S(1)} %get-tuple-element.17), channel_id=1, source_target_pairs={{0,96},{32,128},{64,160},{96,192},{128,224},{160,0},{192,32},{224,... | collective-permute-start | bytes 319496 | tf_op jit(solution)/shard_map/ppermute | solution.py:287
  11.4 7.0 %collective-permute-start.5 = (bf16[208,256]{1,0:T(8,128)(2,1)S(1)}, bf16[208,256]{1,0:T(8,128)(2,1)S(1)}, u32[]{:S(2)}, u32[]{:S(2)}) collective-permute-start(bf16[208,256]{1,0:T(8,128)(2,1)S(1)} %get-tuple-element.18), channel_id=1, source_target_pairs={{0,64},{32,96},{64,128},{96,160},{128,192},{160,224},{192,0},{224,... | collective-permute-start | bytes 319496 | tf_op jit(solution)/shard_map/ppermute | solution.py:287
  13.4 7.1 %collective-permute-start.6 = (bf16[208,256]{1,0:T(8,128)(2,1)S(1)}, bf16[208,256]{1,0:T(8,128)(2,1)S(1)}, u32[]{:S(2)}, u32[]{:S(2)}) collective-permute-start(bf16[208,256]{1,0:T(8,128)(2,1)S(1)} %get-tuple-element.19), channel_id=1, source_target_pairs={{0,32},{32,64},{64,96},{96,128},{128,160},{160,192},{192,224},{224... | collective-permute-start | bytes 319496 | tf_op jit(solution)/shard_map/ppermute | solution.py:287
  32.7 61.8 %copy-start.6 = (bf16[1024,128]{1,0:T(8,128)(2,1)S(1)}, bf16[1024,128]{1,0:T(8,128)(2,1)}, u32[]{:S(2)}) copy-start(bf16[1024,128]{1,0:T(8,128)(2,1)} %w_ref.1) | copy-start | bytes 786436
  32.7 64.5 %all-to-all-start = ((bf16[8,384,256]{2,1,0:T(8,128)(2,1)}), bf16[8,384,256]{2,1,0:T(8,128)(2,1)S(1)}, u32[]{:S(2)}, u32[]{:S(2)}) async-start(bf16[8,384,256]{2,1,0:T(8,128)(2,1)} %get-tuple-element.20), calls=%async_computation | async-start | bytes 3145728 | tf_op jit(solution)/shard_map/all_to_all | solution.py:372
  38.8 29.2 %collective-permute-start.7 = (bf16[96,512]{1,0:T(8,128)(2,1)S(1)}, bf16[96,512]{1,0:T(8,128)(2,1)S(1)}, u32[]{:S(2)}, u32[]{:S(2)}) collective-permute-start(bf16[96,512]{1,0:T(8,128)(2,1)S(1)} %get-tuple-element.21), channel_id=1, source_target_pairs={{0,0},{1,1},{2,2},{3,3},{4,36},{5,37},{6,38},{7,39},{8,64},{9,65},... | collective-permute-start | bytes 294920 | tf_op jit(solution)/shard_map/ppermute | solution.py:326
  45.0 27.7 %collective-permute-start.10 = (bf16[96,512]{1,0:T(8,128)(2,1)S(1)}, bf16[96,512]{1,0:T(8,128)(2,1)S(1)}, u32[]{:S(2)}, u32[]{:S(2)}) collective-permute-start(bf16[96,512]{1,0:T(8,128)(2,1)S(1)} %get-tuple-element.21), channel_id=1, source_target_pairs={{0,24},{1,25},{2,26},{3,27},{4,60},{5,61},{6,62},{7,63},{8,88},{9,... | collective-permute-start | bytes 294920 | tf_op jit(solution)/shard_map/ppermute | solution.py:326
  47.0 25.8 %collective-permute-start.9 = (bf16[96,512]{1,0:T(8,128)(2,1)S(1)}, bf16[96,512]{1,0:T(8,128)(2,1)S(1)}, u32[]{:S(2)}, u32[]{:S(2)}) collective-permute-start(bf16[96,512]{1,0:T(8,128)(2,1)S(1)} %get-tuple-element.21), channel_id=1, source_target_pairs={{0,16},{1,17},{2,18},{3,19},{4,52},{5,53},{6,54},{7,55},{8,80},{9,... | collective-permute-start | bytes 294920 | tf_op jit(solution)/shard_map/ppermute | solution.py:326
  56.3 15.6 %collective-permute-start.8 = (bf16[96,512]{1,0:T(8,128)(2,1)S(1)}, bf16[96,512]{1,0:T(8,128)(2,1)S(1)}, u32[]{:S(2)}, u32[]{:S(2)}) collective-permute-start(bf16[96,512]{1,0:T(8,128)(2,1)S(1)} %get-tuple-element.21), channel_id=1, source_target_pairs={{0,8},{1,9},{2,10},{3,11},{4,44},{5,45},{6,46},{7,47},{8,72},{9,73... | collective-permute-start | bytes 294920 | tf_op jit(solution)/shard_map/ppermute | solution.py:326
  72.8 8.4 %collective-permute-start.16 = (bf16[384,512]{1,0:T(8,128)(2,1)S(1)}, bf16[384,512]{1,0:T(8,128)(2,1)}, u32[]{:S(2)}, u32[]{:S(2)}) collective-permute-start(bf16[384,512]{1,0:T(8,128)(2,1)S(1)} %constant_dynamic-update-slice_fusion.refs_0_), channel_id=1, source_target_pairs={{0,4},{1,5},{2,6},{3,7},{4,0},{5,1},{6,2},{7,3},{8,12},{9,13},{10,... | collective-permute-start | bytes 1179656 | tf_op jit(solution)/shard_map/ppermute | solution.py:329
  72.9 17.5 %collective-permute-start.14 = (bf16[384,512]{1,0:T(8,128)(2,1)S(1)}, bf16[384,512]{1,0:T(8,128)(2,1)}, u32[]{:S(2)}, u32[]{:S(2)}) collective-permute-start(bf16[384,512]{1,0:T(8,128)(2,1)S(1)} %constant_dynamic-update-slice_fusion.refs_0_), channel_id=1, source_target_pairs={{0,6},{1,7},{2,0},{3,1},{4,2},{5,3},{6,4},{7,5},{8,14},{9,15},{10,... | collective-permute-start | bytes 1179656 | tf_op jit(solution)/shard_map/ppermute | solution.py:329
  75.6 16.2 %collective-permute-start.12 = (bf16[384,512]{1,0:T(8,128)(2,1)S(1)}, bf16[384,512]{1,0:T(8,128)(2,1)}, u32[]{:S(2)}, u32[]{:S(2)}) collective-permute-start(bf16[384,512]{1,0:T(8,128)(2,1)S(1)} %constant_dynamic-update-slice_fusion.refs_0_), channel_id=1, source_target_pairs={{0,2},{1,3},{2,4},{3,5},{4,6},{5,7},{6,0},{7,1},{8,10},{9,11},{10,... | collective-permute-start | bytes 1179656 | tf_op jit(solution)/shard_map/ppermute | solution.py:329
  75.6 24.7 %collective-permute-start.11 = (bf16[384,512]{1,0:T(8,128)(2,1)S(1)}, bf16[384,512]{1,0:T(8,128)(2,1)}, u32[]{:S(2)}, u32[]{:S(2)}) collective-permute-start(bf16[384,512]{1,0:T(8,128)(2,1)S(1)} %constant_dynamic-update-slice_fusion.refs_0_), channel_id=1, source_target_pairs={{0,1},{1,0},{2,3},{3,2},{4,5},{5,4},{6,7},{7,6},{8,9},{9,8},{10,11... | collective-permute-start | bytes 1179656 | tf_op jit(solution)/shard_map/ppermute | solution.py:330
  81.2 19.1 %collective-permute-start.17 = (bf16[384,512]{1,0:T(8,128)(2,1)}, bf16[384,512]{1,0:T(8,128)(2,1)}, u32[]{:S(2)}, u32[]{:S(2)}) collective-permute-start(bf16[384,512]{1,0:T(8,128)(2,1)} %collective-permute-done.16.refs_6_), channel_id=1, source_target_pairs={{0,1},{1,0},{2,3},{3,2},{4,5},{5,4},{6,7},{7,6},{8,9},{9,8},{10,11... | collective-permute-start | bytes 1179656 | tf_op jit(solution)/shard_map/ppermute | solution.py:330
  90.4 9.9 %collective-permute-start.15 = (bf16[384,512]{1,0:T(8,128)(2,1)}, bf16[384,512]{1,0:T(8,128)(2,1)}, u32[]{:S(2)}, u32[]{:S(2)}) collective-permute-start(bf16[384,512]{1,0:T(8,128)(2,1)} %collective-permute-done.14.refs_4_), channel_id=1, source_target_pairs={{0,1},{1,0},{2,3},{3,2},{4,5},{5,4},{6,7},{7,6},{8,9},{9,8},{10,11... | collective-permute-start | bytes 1179656 | tf_op jit(solution)/shard_map/ppermute | solution.py:330
  91.8 8.5 %collective-permute-start.13 = (bf16[384,512]{1,0:T(8,128)(2,1)}, bf16[384,512]{1,0:T(8,128)(2,1)}, u32[]{:S(2)}, u32[]{:S(2)}) collective-permute-start(bf16[384,512]{1,0:T(8,128)(2,1)} %collective-permute-done.12.refs_2_), channel_id=1, source_target_pairs={{0,1},{1,0},{2,3},{3,2},{4,5},{5,4},{6,7},{7,6},{8,9},{9,8},{10,11... | collective-permute-start | bytes 1179656 | tf_op jit(solution)/shard_map/ppermute | solution.py:330
  (13 other events, 122.5 us)
